TPU v7x, 256 devices: a whole 4x4x8 slice. The times are simulated.
256 devices in a mesh: dx: 8 (over z_lo, y), dy: 32 (over z_hi, x, core).
Axes of the slice: x: 4, y: 4, z: 8 (z_hi: 4, z_lo: 2; z = z_hi * 2 + z_lo), core: 2. Of those that a mesh axis runs over, the one named last changes fastest.
Arguments:
- vectors: bfloat16 [2, 64, 512, 16, 128], P(None, 'dx', 'dy'), may hold values from -6 to 6
- resident: bfloat16 [64, 512, 16, 512], P('dx', 'dy'), may hold values from -6 to 6
- inv_mass: float32 [64, 512, 16], P('dx', 'dy'), may hold values from 0.26 to 1.3
- potential: float32 [64, 512, 16], P('dx', 'dy'), may hold values from -0.4 to 0.4
- cell_matrix: bfloat16 [729, 729], replicated, may hold values from -1 to 1.3, as said below
- connectivity: int32 [8, 32, 4, 729], P('dx', 'dy'), may hold values from 0 to 2447, as said below
Outputs:
- filtered: float32 [2, 64, 512, 16, 128], P(None, 'dx', 'dy')
- margin: float32 [512, 256], P('dy')
Inputs may be any that keep to these rules, and one draw needn't show every extreme that they name: `connectivity`: cell c of a device, with c = (cx * 2 + cy) * 2 + cz, covers the extended nodes with i from cx * 8 to cx * 8 + 8, j from cy * 8 to cy * 8 + 8, and k from cz * 8 to cz * 8 + 8 taken modulo 2 * 8; its 729 entries name each of these nodes once, in an order that may differ from cell to cell. `cell_matrix`: Symmetric.
All inputs are finite; a program needn't handle non-finite values.
Results may differ from a plain program's by a relative error of at most 0.0055.
Values may be sent and summed in bfloat16 or wider, within the bound.
A program may use at most 64 MiB of HBM per device.

v0:
```python
import math

import jax
import jax.numpy as jnp
from jax import lax
from jax.sharding import PartitionSpec as P

BLOCKS = 2
DEGREE = 3


center_shift = 1.2
half_width = 2.0


def from_behind(value, axis, steps):
    count = lax.axis_size(axis)
    pairs = [(source, (source + steps) % count) for source in range(count)]
    return lax.ppermute(value, axis, pairs)


def cut_along(value, dim, length):
    lengths = value.shape
    pieces = value.reshape(*lengths[:dim], length, lengths[dim] // length, *lengths[dim + 1 :])
    return jnp.moveaxis(pieces, dim, 0)


def sum_at_owner(value, axis, dim):
    length = lax.axis_size(axis)
    pieces = lax.all_to_all(cut_along(value, dim, length), axis, 0, 0, tiled=True)
    return jnp.sum(pieces, axis=0)


def sent_to_all(value, axis):
    length = lax.axis_size(axis)
    return lax.all_to_all(
        jnp.broadcast_to(value[None], (length, *value.shape)), axis, 0, 0, tiled=True
    )


def taken_together(value, axis):
    return sent_to_all(value, axis).sum(axis=0)


def body(vectors, resident, inv_mass, potential, cell_matrix, connectivity):
    node_index = connectivity.reshape(-1)
    cell_count = connectivity.shape[2]
    node_count = connectivity.shape[3]
    extent_x, extent_y, extent_z = inv_mass.shape
    ext_rows = (extent_x + 1) * (extent_y + 1) * extent_z
    total_nodes = extent_x * extent_y * extent_z * lax.axis_size("dx") * lax.axis_size("dy")
    norm_scale = 1.0 / math.sqrt(total_nodes)
    resident_rows = resident.reshape(-1, resident.shape[-1])

    def apply_hamiltonian(values):
        vec_width = values.shape[-1]
        scaled = (values * inv_mass[..., None]).astype(jnp.bfloat16)
        upper_x = from_behind(scaled[:1], "dx", -1)
        grown = jnp.concatenate([scaled, upper_x], axis=0)
        upper_y = from_behind(grown[:, :1], "dy", -1)
        grown = jnp.concatenate([grown, upper_y], axis=1)
        picked = jnp.take(grown.reshape(-1, vec_width), node_index, axis=0).reshape(
            cell_count, node_count, vec_width
        )
        product = jnp.einsum("il,clw->ciw", cell_matrix, picked, preferred_element_type=jnp.float32)
        summed = jax.ops.segment_sum(
            product.reshape(-1, vec_width), node_index, num_segments=ext_rows
        )
        summed = summed.reshape(extent_x + 1, extent_y + 1, extent_z, vec_width)
        from_lower_y = from_behind(summed[:, extent_y:], "dy", 1)
        folded = summed[:, :extent_y].at[:, 0:1].add(from_lower_y)
        from_lower_x = from_behind(folded[extent_x:], "dx", 1)
        folded = folded[:extent_x].at[0:1].add(from_lower_x)
        return inv_mass[..., None] * folded + potential[..., None] * values

    stacked = jnp.concatenate([vectors[block_id] for block_id in range(BLOCKS)], axis=-1).astype(
        jnp.float32
    )
    image = apply_hamiltonian(stacked)
    older = stacked
    current = (image - center_shift * stacked) / half_width
    for degree_id in range(1, DEGREE):
        image = apply_hamiltonian(current)
        newer = 2.0 * (image - center_shift * current) / half_width - older
        older = current
        current = newer
    vec_width = current.shape[-1]
    rounded = current.astype(jnp.bfloat16).reshape(-1, vec_width)
    local = lax.dot_general(
        resident_rows, rounded, (((0,), (0,)), ((), ())), preferred_element_type=jnp.float32
    )
    local = local * norm_scale
    owned_rows = sum_at_owner(local, "dy", 0)
    margin = taken_together(owned_rows, "dx")
    filtered = jnp.stack(jnp.split(current, BLOCKS, axis=-1))
    return (filtered, margin)


def solution(mesh):
    return jax.shard_map(
        body,
        mesh=mesh,
        in_specs=(
            P(None, "dx", "dy", None, None),
            P("dx", "dy", None, None),
            P("dx", "dy", None),
            P("dx", "dy", None),
            P(),
            P("dx", "dy", None, None),
        ),
        out_specs=(P(None, "dx", "dy", None, None), P("dy", None)),
        check_vma=False,
    )
```

profile of v0, /device:TPU:4, one launch (start us, length us, event | category | flops | bytes accessed | tf_op | source)
XLA Modules:
  0.0 261.6 jit_solution(2299564943875757439)
XLA Ops:
  0.7 1.5 slice_bitcast_fusion.3
  3.4 4.4 %collective-permute-start = (bf16[1,16,16,256]{3,2,1,0:T(8,128)(2,1)S(1)}, bf16[1,16,16,256]{3,2,1,0:T(8,128)(2,1)S(1)}, u32[]{:S(2)}, u32[]{:S(2)}) collective-permute-start(bf16[1,16,16,256]{3,2,1,0:T(8,128)(2,1)S(1)} %slice.272), channel_id=1, source_target_pairs={{0,224},{32,0},{64,32},{96,64},{128,96},{160,128},{192,160},{224,1... | collective-permute-start | bytes 393224 | tf_op jit(solution)/shard_map/ppermute | solution.py:19
  8.0 2.6 %collective-permute-done = bf16[1,16,16,256]{3,2,1,0:T(8,128)(2,1)S(1)} collective-permute-done((bf16[1,16,16,256]{3,2,1,0:T(8,128)(2,1)S(1)}, bf16[1,16,16,256]{3,2,1,0:T(8,128)(2,1)S(1)}, u32[]{:S(2)}, u32[]{:S(2)}) %collective-permute-start) | collective-permute-done | bytes 131104 | tf_op jit(solution)/shard_map/ppermute | solution.py:19
  11.3 1.4 collective-permute-done.1
  12.7 1.4 pad_maximum_fusion.1
  14.1 9.7 %gather_fusion = bf16[2916,256]{1,0:T(8,128)(2,1)} fusion(bf16[2448,256]{1,0:T(8,128)(2,1)S(1)} %bitcast.43, s32[3072]{0:T(1024)} %pad_clamp_fusion), kind=kCustom, calls=%fused_computation.clone | custom fusion | bytes 2997648 | tf_op jit(solution)/shard_map/jit(_take)/gather | solution.py:62
  23.7 3.5 %broadcast_select_fusion = bf16[2916,256]{1,0:T(8,128)(2,1)} fusion(bf16[2916,256]{1,0:T(8,128)(2,1)} %gather_fusion, pred[2916]{0:T(1024)(128)(4,1)S(1)} %compare_and_fusion), kind=kLoop, calls=%fused_computation.20 | loop fusion | flops 746496 | bytes 2988900 | tf_op jit(solution)/shard_map/jit(_take)/select_n | solution.py:62
  27.2 3.0 %reshape.261 = bf16[4,729,256]{2,1,0:T(8,128)(2,1)} reshape(bf16[2916,256]{1,0:T(8,128)(2,1)} %broadcast_select_fusion) | data formatting | bytes 2985984 | tf_op jit(solution)/shard_map/reshape | solution.py:62
  30.2 4.4 %convolution_bitcast_fusion.2 = f32[4,729,256]{2,1,0:T(8,128)} fusion(bf16[4,729,256]{2,1,0:T(8,128)(2,1)} %reshape.261, bf16[729,729]{1,0:T(8,128)(2,1)S(1)} %copy-done.21), kind=kOutput, calls=%fused_computation.19 | convolution fusion | flops 1088391168 | bytes 5541858 | tf_op jit(solution)/shard_map/il,clw->ciw/dot_general | solution.py:65
  34.6 3.9 %reshape.301 = f32[2916,256]{1,0:T(8,128)} reshape(f32[4,729,256]{2,1,0:T(8,128)} %convolution_bitcast_fusion.2) | data formatting | bytes 5971968 | tf_op jit(solution)/shard_map/reshape | solution.py:67
  38.5 17.5 %scatter_custom_fusion = f32[2448,256]{1,0:T(8,128)} fusion(s32[2916]{0:T(1024)} %copy-done.19, f32[2916,256]{1,0:T(8,128)} %reshape.301, f32[]{:T(128)} %constant.152.clone.1), kind=kCustom, calls=%fused_computation.30 | custom fusion | flops 746496 | bytes 2507264 | tf_op jit(solution)/shard_map/scatter-add | solution.py:66
  56.9 1.4 collective-permute-start.2
  58.3 1.9 slice.273
  60.2 1.4 collective-permute-done.2
  62.9 9.7 %collective-permute-done.3 = f32[1,16,16,256]{3,2,1,0:T(8,128)S(1)} collective-permute-done((f32[1,16,16,256]{3,2,1,0:T(8,128)S(1)}, f32[1,16,16,256]{3,2,1,0:T(8,128)S(1)}, u32[]{:S(2)}, u32[]{:S(2)}) %collective-permute-start.3) | collective-permute-done | bytes 262176 | tf_op jit(solution)/shard_map/ppermute | solution.py:19
  72.6 1.0 multiply_convert_fusion.1
  73.9 2.0 collective-permute-start.4
  75.9 3.2 %collective-permute-done.4 = bf16[1,16,16,256]{3,2,1,0:T(8,128)(2,1)S(1)} collective-permute-done((bf16[1,16,16,256]{3,2,1,0:T(8,128)(2,1)S(1)}, bf16[1,16,16,256]{3,2,1,0:T(8,128)(2,1)S(1)}, u32[]{:S(2)}, u32[]{:S(2)}) %collective-permute-start.4) | collective-permute-done | bytes 131104 | tf_op jit(solution)/shard_map/ppermute | solution.py:19
  79.3 2.0 collective-permute-done.5
  81.4 9.5 %gather_fusion.1 = bf16[2916,256]{1,0:T(8,128)(2,1)} fusion(bf16[2448,256]{1,0:T(8,128)(2,1)S(1)} %bitcast.44, s32[3072]{0:T(1024)S(1)} %copy-done.18), kind=kCustom, calls=%fused_computation.1.clone | custom fusion | bytes 2997648 | tf_op jit(solution)/shard_map/jit(_take)/gather | solution.py:62
  90.9 3.5 %broadcast_select_fusion.1 = bf16[2916,256]{1,0:T(8,128)(2,1)} fusion(bf16[2916,256]{1,0:T(8,128)(2,1)} %gather_fusion.1, pred[2916]{0:T(1024)(128)(4,1)S(1)} %compare_and_fusion), kind=kLoop, calls=%fused_computation.21 | loop fusion | flops 746496 | bytes 2988900 | tf_op jit(solution)/shard_map/jit(_take)/select_n | solution.py:62
  94.4 3.0 %reshape.265 = bf16[4,729,256]{2,1,0:T(8,128)(2,1)} reshape(bf16[2916,256]{1,0:T(8,128)(2,1)} %broadcast_select_fusion.1) | data formatting | bytes 2985984 | tf_op jit(solution)/shard_map/reshape | solution.py:62
  97.5 4.3 %convolution_bitcast_fusion.1 = f32[4,729,256]{2,1,0:T(8,128)} fusion(bf16[4,729,256]{2,1,0:T(8,128)(2,1)} %reshape.265, bf16[729,729]{1,0:T(8,128)(2,1)S(1)} %copy-done.22), kind=kOutput, calls=%fused_computation.18 | convolution fusion | flops 1088391168 | bytes 5541858 | tf_op jit(solution)/shard_map/il,clw->ciw/dot_general | solution.py:65
  101.8 3.9 %reshape.309 = f32[2916,256]{1,0:T(8,128)} reshape(f32[4,729,256]{2,1,0:T(8,128)} %convolution_bitcast_fusion.1) | data formatting | bytes 5971968 | tf_op jit(solution)/shard_map/reshape | solution.py:67
  105.7 17.4 %scatter_custom_fusion.1 = f32[2448,256]{1,0:T(8,128)} fusion(s32[2916]{0:T(1024)} %copy-done.19, f32[2916,256]{1,0:T(8,128)} %reshape.309, f32[]{:T(128)} %constant.152.clone.1), kind=kCustom, calls=%fused_computation.28 | custom fusion | flops 746496 | bytes 2507264 | tf_op jit(solution)/shard_map/scatter-add | solution.py:66
  124.1 4.6 %collective-permute-start.6 = (f32[9,1,16,256]{3,2,1,0:T(8,128)S(1)}, f32[9,1,16,256]{3,2,1,0:T(8,128)S(1)}, u32[]{:S(2)}, u32[]{:S(2)}) collective-permute-start(f32[9,1,16,256]{3,2,1,0:T(8,128)S(1)} %slice.282), channel_id=1, source_target_pairs={{0,1},{1,2},{2,3},{3,4},{4,5},{5,6},{6,7},{7,8},{8,9},{9,10},{10,1... | collective-permute-start | bytes 442376 | tf_op jit(solution)/shard_map/ppermute | solution.py:19
  128.6 1.9 slice.280
  131.8 10.6 %collective-permute-done.7 = f32[1,16,16,256]{3,2,1,0:T(8,128)S(1)} collective-permute-done((f32[1,16,16,256]{3,2,1,0:T(8,128)S(1)}, f32[1,16,16,256]{3,2,1,0:T(8,128)S(1)}, u32[]{:S(2)}, u32[]{:S(2)}) %collective-permute-start.7) | collective-permute-done | bytes 262176 | tf_op jit(solution)/shard_map/ppermute | solution.py:19
  142.5 1.1 multiply_convert_fusion
  143.8 1.8 collective-permute-start.8
  145.6 3.3 %collective-permute-done.8 = bf16[1,16,16,256]{3,2,1,0:T(8,128)(2,1)S(1)} collective-permute-done((bf16[1,16,16,256]{3,2,1,0:T(8,128)(2,1)S(1)}, bf16[1,16,16,256]{3,2,1,0:T(8,128)(2,1)S(1)}, u32[]{:S(2)}, u32[]{:S(2)}) %collective-permute-start.8) | collective-permute-done | bytes 131104 | tf_op jit(solution)/shard_map/ppermute | solution.py:19
  149.2 2.0 collective-permute-done.9
  151.3 9.7 %gather_fusion.2 = bf16[2916,256]{1,0:T(8,128)(2,1)} fusion(bf16[2448,256]{1,0:T(8,128)(2,1)S(1)} %bitcast.42, s32[3072]{0:T(1024)} %pad_clamp_fusion), kind=kCustom, calls=%fused_computation.2.clone | custom fusion | bytes 2997648 | tf_op jit(solution)/shard_map/jit(_take)/gather | solution.py:62
  161.0 3.5 %broadcast_select_fusion.2 = bf16[2916,256]{1,0:T(8,128)(2,1)} fusion(bf16[2916,256]{1,0:T(8,128)(2,1)} %gather_fusion.2, pred[2916]{0:T(1024)(128)(4,1)S(1)} %compare_and_fusion), kind=kLoop, calls=%fused_computation.22 | loop fusion | flops 746496 | bytes 2988900 | tf_op jit(solution)/shard_map/jit(_take)/select_n | solution.py:62
  164.5 3.0 %reshape.269 = bf16[4,729,256]{2,1,0:T(8,128)(2,1)} reshape(bf16[2916,256]{1,0:T(8,128)(2,1)} %broadcast_select_fusion.2) | data formatting | bytes 2985984 | tf_op jit(solution)/shard_map/reshape | solution.py:62
  167.5 4.4 %convolution_bitcast_fusion = f32[4,729,256]{2,1,0:T(8,128)} fusion(bf16[4,729,256]{2,1,0:T(8,128)(2,1)} %reshape.269, bf16[729,729]{1,0:T(8,128)(2,1)S(1)} %copy-done.23), kind=kOutput, calls=%fused_computation.17 | convolution fusion | flops 1088391168 | bytes 5541858 | tf_op jit(solution)/shard_map/il,clw->ciw/dot_general | solution.py:65
  171.9 3.9 %reshape.317 = f32[2916,256]{1,0:T(8,128)} reshape(f32[4,729,256]{2,1,0:T(8,128)} %convolution_bitcast_fusion) | data formatting | bytes 5971968 | tf_op jit(solution)/shard_map/reshape | solution.py:67
  175.8 17.5 %scatter_custom_fusion.2 = f32[2448,256]{1,0:T(8,128)} fusion(s32[2916]{0:T(1024)} %copy-done.19, f32[2916,256]{1,0:T(8,128)} %reshape.317, f32[]{:T(128)} %constant.152.clone.1), kind=kCustom, calls=%fused_computation.26 | custom fusion | flops 746496 | bytes 2507264 | tf_op jit(solution)/shard_map/scatter-add | solution.py:66
  194.2 4.6 %collective-permute-start.10 = (f32[9,1,16,256]{3,2,1,0:T(8,128)S(1)}, f32[9,1,16,256]{3,2,1,0:T(8,128)S(1)}, u32[]{:S(2)}, u32[]{:S(2)}) collective-permute-start(f32[9,1,16,256]{3,2,1,0:T(8,128)S(1)} %slice.289), channel_id=1, source_target_pairs={{0,1},{1,2},{2,3},{3,4},{4,5},{5,6},{6,7},{7,8},{8,9},{9,10},{10,1... | collective-permute-start | bytes 442376 | tf_op jit(solution)/shard_map/ppermute | solution.py:19
  198.8 1.9 slice.287
  202.8 9.5 %collective-permute-done.11 = f32[1,16,16,256]{3,2,1,0:T(8,128)S(1)} collective-permute-done((f32[1,16,16,256]{3,2,1,0:T(8,128)S(1)}, f32[1,16,16,256]{3,2,1,0:T(8,128)S(1)}, u32[]{:S(2)}, u32[]{:S(2)}) %collective-permute-start.11) | collective-permute-done | bytes 262176 | tf_op jit(solution)/shard_map/ppermute | solution.py:19
  212.4 1.7 multiply_subtract_fusion
  214.1 1.3 copy-done.15
  216.4 34.0 %all_to_all.10 = f32[32,16,256]{2,1,0:T(8,128)S(1)} all-to-all(f32[32,16,256]{2,1,0:T(8,128)S(1)} %bitcast.54), channel_id=1, replica_groups=mesh['dx'=8,'dy'=32] {'dy'}, dimensions={0} | all-to-all | bytes 1048576 | tf_op jit(solution)/shard_map/all_to_all | solution.py:30
  251.1 3.4 %all-to-all-start.1 = ((f32[8,16,256]{2,1,0:T(8,128)}), f32[8,16,256]{2,1,0:T(8,128)S(1)}, u32[]{:S(2)}, u32[]{:S(2)}) async-start(f32[8,16,256]{2,1,0:T(8,128)} %broadcast_in_dim.11), calls=%async_computation.1 | async-start | bytes 262144 | tf_op jit(solution)/shard_map/all_to_all | solution.py:36
  254.5 1.7 slice_bitcast_fusion.1
  256.1 1.5 pad_maximum_fusion
  257.6 3.4 %all-to-all-done.1 = f32[8,16,256]{2,1,0:T(8,128)S(1)} async-done(((f32[8,16,256]{2,1,0:T(8,128)}), f32[8,16,256]{2,1,0:T(8,128)S(1)}, u32[]{:S(2)}, u32[]{:S(2)}) %all-to-all-start.1) | async-done | bytes 131104 | tf_op jit(solution)/shard_map/all_to_all | solution.py:36
  (90 shorter events, 12.8 us)
Async XLA Ops:
  0.6 214.8 %copy-start = (bf16[8,16,16,512]{3,2,1,0:T(8,128)(2,1)S(1)}, bf16[8,16,16,512]{3,2,1,0:T(8,128)(2,1)}, u32[]{:S(2)}) copy-start(bf16[8,16,16,512]{3,2,1,0:T(8,128)(2,1)} %param.21) | copy-start | bytes 6291460
  0.6 2.4 copy-start.16
  0.7 7.2 %copy-start.20 = (s32[1,1,4,729]{3,2,1,0:T(4,128)S(1)}, s32[1,1,4,729]{3,2,1,0:T(4,128)}, u32[]{:S(2)}) copy-start(s32[1,1,4,729]{3,2,1,0:T(4,128)} %param.25) | copy-start | bytes 34996
  2.2 0.8 copy-start.6
  2.2 1.1 copy-start.10
  3.4 7.9 %copy-start.14 = (bf16[8,16,16,256]{3,2,1,0:T(8,128)(2,1)}, bf16[8,16,16,256]{3,2,1,0:T(8,128)(2,1)S(1)}, u32[]{:S(2)}) copy-start(bf16[8,16,16,256]{3,2,1,0:T(8,128)(2,1)S(1)} %fusion) | copy-start | bytes 3145732
  3.4 7.2 %collective-permute-start = (bf16[1,16,16,256]{3,2,1,0:T(8,128)(2,1)S(1)}, bf16[1,16,16,256]{3,2,1,0:T(8,128)(2,1)S(1)}, u32[]{:S(2)}, u32[]{:S(2)}) collective-permute-start(bf16[1,16,16,256]{3,2,1,0:T(8,128)(2,1)S(1)} %slice.272), channel_id=1, source_target_pairs={{0,224},{32,0},{64,32},{96,64},{128,96},{160,128},{192,160},{224,1... | collective-permute-start | bytes 393224 | tf_op jit(solution)/shard_map/ppermute | solution.py:19
  7.9 3.4 %copy-start.19 = (s32[2916]{0:T(1024)}, s32[2916]{0:T(1024)S(1)}, u32[]{:S(2)}) copy-start(s32[2916]{0:T(1024)S(1)} %reshape.315) | copy-start | bytes 34996
  10.6 2.1 collective-permute-start.1
  27.2 3.0 %copy-start.21 = (bf16[729,729]{1,0:T(8,128)(2,1)S(1)}, bf16[729,729]{1,0:T(8,128)(2,1)}, u32[]{:S(2)}) copy-start(bf16[729,729]{1,0:T(8,128)(2,1)} %param.24) | copy-start | bytes 3188650
  56.9 4.7 %collective-permute-start.2 = (f32[9,1,16,256]{3,2,1,0:T(8,128)S(1)}, f32[9,1,16,256]{3,2,1,0:T(8,128)S(1)}, u32[]{:S(2)}, u32[]{:S(2)}) collective-permute-start(f32[9,1,16,256]{3,2,1,0:T(8,128)S(1)} %slice.275), channel_id=1, source_target_pairs={{0,1},{1,2},{2,3},{3,4},{4,5},{5,6},{6,7},{7,8},{8,9},{9,10},{10,1... | collective-permute-start | bytes 442376 | tf_op jit(solution)/shard_map/ppermute | solution.py:19
  62.5 10.0 %collective-permute-start.3 = (f32[1,16,16,256]{3,2,1,0:T(8,128)S(1)}, f32[1,16,16,256]{3,2,1,0:T(8,128)S(1)}, u32[]{:S(2)}, u32[]{:S(2)}) collective-permute-start(f32[1,16,16,256]{3,2,1,0:T(8,128)S(1)} %slice.278), channel_id=1, source_target_pairs={{0,32},{32,64},{64,96},{96,128},{128,160},{160,192},{192,224},{224... | collective-permute-start | bytes 786440 | tf_op jit(solution)/shard_map/ppermute | solution.py:19
  62.6 9.9 %copy-start.7 = (bf16[8,16,16,128]{3,2,1,0:T(8,128)(2,1)S(1)}, bf16[8,16,16,128]{3,2,1,0:T(8,128)(2,1)}, u32[]{:S(2)}) copy-start(bf16[8,16,16,128]{3,2,1,0:T(8,128)(2,1)} %copy-done.6) | copy-start | bytes 1572868
  62.7 9.9 %copy-start.11 = (bf16[8,16,16,128]{3,2,1,0:T(8,128)(2,1)S(1)}, bf16[8,16,16,128]{3,2,1,0:T(8,128)(2,1)}, u32[]{:S(2)}) copy-start(bf16[8,16,16,128]{3,2,1,0:T(8,128)(2,1)} %copy-done.10) | copy-start | bytes 1572868
  62.7 9.9 %copy-start.17 = (f32[8,16,16]{2,1,0:T(8,128)S(1)}, f32[8,16,16]{2,1,0:T(8,128)}, u32[]{:S(2)}) copy-start(f32[8,16,16]{2,1,0:T(8,128)} %param.23) | copy-start | bytes 24580
  72.6 1.3 copy-start.1
  73.9 7.5 %copy-start.18 = (s32[3072]{0:T(1024)S(1)}, s32[3072]{0:T(1024)}, u32[]{:S(2)}) copy-start(s32[3072]{0:T(1024)} %pad_clamp_fusion) | copy-start | bytes 36868
  73.9 5.2 %collective-permute-start.4 = (bf16[1,16,16,256]{3,2,1,0:T(8,128)(2,1)S(1)}, bf16[1,16,16,256]{3,2,1,0:T(8,128)(2,1)S(1)}, u32[]{:S(2)}, u32[]{:S(2)}) collective-permute-start(bf16[1,16,16,256]{3,2,1,0:T(8,128)(2,1)S(1)} %slice.279), channel_id=1, source_target_pairs={{0,224},{32,0},{64,32},{96,64},{128,96},{160,128},{192,160},{224,1... | collective-permute-start | bytes 393224 | tf_op jit(solution)/shard_map/ppermute | solution.py:19
  79.2 2.1 collective-permute-start.5
  94.4 3.0 %copy-start.22 = (bf16[729,729]{1,0:T(8,128)(2,1)S(1)}, bf16[729,729]{1,0:T(8,128)(2,1)}, u32[]{:S(2)}) copy-start(bf16[729,729]{1,0:T(8,128)(2,1)} %param.24) | copy-start | bytes 3188650
  124.1 6.5 %collective-permute-start.6 = (f32[9,1,16,256]{3,2,1,0:T(8,128)S(1)}, f32[9,1,16,256]{3,2,1,0:T(8,128)S(1)}, u32[]{:S(2)}, u32[]{:S(2)}) collective-permute-start(f32[9,1,16,256]{3,2,1,0:T(8,128)S(1)} %slice.282), channel_id=1, source_target_pairs={{0,1},{1,2},{2,3},{3,4},{4,5},{5,6},{6,7},{7,8},{8,9},{9,10},{10,1... | collective-permute-start | bytes 442376 | tf_op jit(solution)/shard_map/ppermute | solution.py:19
  131.5 10.9 %collective-permute-start.7 = (f32[1,16,16,256]{3,2,1,0:T(8,128)S(1)}, f32[1,16,16,256]{3,2,1,0:T(8,128)S(1)}, u32[]{:S(2)}, u32[]{:S(2)}) collective-permute-start(f32[1,16,16,256]{3,2,1,0:T(8,128)S(1)} %slice.285), channel_id=1, source_target_pairs={{0,32},{32,64},{64,96},{96,128},{128,160},{160,192},{192,224},{224... | collective-permute-start | bytes 786440 | tf_op jit(solution)/shard_map/ppermute | solution.py:19
  131.6 10.8 %copy-start.2 = (f32[8,16,16,256]{3,2,1,0:T(8,128)S(1)}, f32[8,16,16,256]{3,2,1,0:T(8,128)}, u32[]{:S(2)}) copy-start(f32[8,16,16,256]{3,2,1,0:T(8,128)} %copy-done.1) | copy-start | bytes 6291460
  131.6 10.8 %copy-start.8 = (bf16[8,16,16,128]{3,2,1,0:T(8,128)(2,1)S(1)}, bf16[8,16,16,128]{3,2,1,0:T(8,128)(2,1)}, u32[]{:S(2)}) copy-start(bf16[8,16,16,128]{3,2,1,0:T(8,128)(2,1)} %copy-done.6) | copy-start | bytes 1572868
  131.6 10.8 %copy-start.12 = (bf16[8,16,16,128]{3,2,1,0:T(8,128)(2,1)S(1)}, bf16[8,16,16,128]{3,2,1,0:T(8,128)(2,1)}, u32[]{:S(2)}) copy-start(bf16[8,16,16,128]{3,2,1,0:T(8,128)(2,1)} %copy-done.10) | copy-start | bytes 1572868
  142.5 1.3 copy-start.4
  143.8 5.1 %collective-permute-start.8 = (bf16[1,16,16,256]{3,2,1,0:T(8,128)(2,1)S(1)}, bf16[1,16,16,256]{3,2,1,0:T(8,128)(2,1)S(1)}, u32[]{:S(2)}, u32[]{:S(2)}) collective-permute-start(bf16[1,16,16,256]{3,2,1,0:T(8,128)(2,1)S(1)} %slice.286), channel_id=1, source_target_pairs={{0,224},{32,0},{64,32},{96,64},{128,96},{160,128},{192,160},{224,1... | collective-permute-start | bytes 393224 | tf_op jit(solution)/shard_map/ppermute | solution.py:19
  148.9 2.3 collective-permute-start.9
  164.5 3.0 %copy-start.23 = (bf16[729,729]{1,0:T(8,128)(2,1)S(1)}, bf16[729,729]{1,0:T(8,128)(2,1)}, u32[]{:S(2)}) copy-start(bf16[729,729]{1,0:T(8,128)(2,1)} %param.24) | copy-start | bytes 3188650
  194.2 7.3 %collective-permute-start.10 = (f32[9,1,16,256]{3,2,1,0:T(8,128)S(1)}, f32[9,1,16,256]{3,2,1,0:T(8,128)S(1)}, u32[]{:S(2)}, u32[]{:S(2)}) collective-permute-start(f32[9,1,16,256]{3,2,1,0:T(8,128)S(1)} %slice.289), channel_id=1, source_target_pairs={{0,1},{1,2},{2,3},{3,4},{4,5},{5,6},{6,7},{7,8},{8,9},{9,10},{10,1... | collective-permute-start | bytes 442376 | tf_op jit(solution)/shard_map/ppermute | solution.py:19
  202.5 9.9 %copy-start.13 = (bf16[8,16,16,128]{3,2,1,0:T(8,128)(2,1)S(1)}, bf16[8,16,16,128]{3,2,1,0:T(8,128)(2,1)}, u32[]{:S(2)}) copy-start(bf16[8,16,16,128]{3,2,1,0:T(8,128)(2,1)} %copy-done.10) | copy-start | bytes 1572868
  202.5 9.9 %copy-start.3 = (f32[8,16,16,256]{3,2,1,0:T(8,128)S(1)}, f32[8,16,16,256]{3,2,1,0:T(8,128)}, u32[]{:S(2)}) copy-start(f32[8,16,16,256]{3,2,1,0:T(8,128)} %copy-done.1) | copy-start | bytes 6291460
  202.5 9.9 %copy-start.5 = (f32[8,16,16,256]{3,2,1,0:T(8,128)S(1)}, f32[8,16,16,256]{3,2,1,0:T(8,128)}, u32[]{:S(2)}) copy-start(f32[8,16,16,256]{3,2,1,0:T(8,128)} %copy-done.4) | copy-start | bytes 6291460
  202.5 9.9 %copy-start.9 = (bf16[8,16,16,128]{3,2,1,0:T(8,128)(2,1)S(1)}, bf16[8,16,16,128]{3,2,1,0:T(8,128)(2,1)}, u32[]{:S(2)}) copy-start(bf16[8,16,16,128]{3,2,1,0:T(8,128)(2,1)} %copy-done.6) | copy-start | bytes 1572868
  202.5 9.8 %collective-permute-start.11 = (f32[1,16,16,256]{3,2,1,0:T(8,128)S(1)}, f32[1,16,16,256]{3,2,1,0:T(8,128)S(1)}, u32[]{:S(2)}, u32[]{:S(2)}) collective-permute-start(f32[1,16,16,256]{3,2,1,0:T(8,128)S(1)} %slice.292), channel_id=1, source_target_pairs={{0,32},{32,64},{64,96},{96,128},{128,160},{160,192},{192,224},{224... | collective-permute-start | bytes 786440 | tf_op jit(solution)/shard_map/ppermute | solution.py:19
  214.1 1.3 copy-start.15
  251.1 9.9 %all-to-all-start.1 = ((f32[8,16,256]{2,1,0:T(8,128)}), f32[8,16,256]{2,1,0:T(8,128)S(1)}, u32[]{:S(2)}, u32[]{:S(2)}) async-start(f32[8,16,256]{2,1,0:T(8,128)} %broadcast_in_dim.11), calls=%async_computation.1 | async-start | bytes 262144 | tf_op jit(solution)/shard_map/all_to_all | solution.py:36
where the time goes:
time: 265 us; the launch traced here: 262 us
  other arithmetic  74.4 us (28%)
  local copies, waits for them, and re-layouts  65.4 us (25%)
  waiting for transfers between devices  49.8 us (19%)
  blocking collectives  34 us (13%)
  starting transfers between devices  23 us (9%)
  matrix products  13.8 us (5%)
    scatter-add x3, other arithmetic, apply_hamiltonian(): jax.ops.segment_sum(product.reshape(-1, vec_width), node_index, num_segme...  52.4 us
    ppermute x12, waiting for transfers between devices, from_behind(): return lax.ppermute(value, axis, pairs)  46.5 us
    all_to_all x1, blocking collectives, sum_at_owner(): lax.all_to_all(cut_along(value, dim, length), axis, 0, 0, tiled=True)  34 us
    gather x3, local copies, waits for them, and re-layouts, apply_hamiltonian(): jnp.take(grown.reshape(-1, vec_width), node_index, axis=0)  28.9 us
    ppermute x12, starting transfers between devices, from_behind(): return lax.ppermute(value, axis, pairs)  19.6 us
    dot_general x3, matrix products, apply_hamiltonian(): jnp.einsum('il,clw->ciw', cell_matrix, picked, preferred_element_type=jnp...  13.1 us
    reshape x3, local copies, waits for them, and re-layouts, apply_hamiltonian(): product.reshape(-1, vec_width)  11.7 us
    select_n x4, other arithmetic, apply_hamiltonian(): jnp.take(grown.reshape(-1, vec_width), node_index, axis=0)  10.5 us
  transfers between devices with their start and end apart: 13, of which 12 were waited for; matrix products, arithmetic and copies ran while one was open for 4% of the time, Pallas kernels for 0%

commit v1 on v0

v1 whole, which is shorter than its diff:
```python
import math

import jax
import jax.numpy as jnp
from jax import lax
from jax.experimental import pallas as pl
from jax.experimental.pallas import tpu as pltpu
from jax.sharding import PartitionSpec as P

MESH = pl.DeviceIdType.MESH
BLOCKS = 2
DEGREE = 3
NCELL = 4
KP = 768
LO, EX, EY, EZ = 8, 9, 17, 16
W = 128
center_shift = 1.2
half_width = 2.0
ZL, NYC = 2, 4
ZH, NXC, CORES = 4, 4, 2
F32, BF16 = jnp.float32, jnp.bfloat16


def kernel(
    norm_scale, vec, res, coef, pos, amat, out, margin,
    ac, acc, uf, y, im, bt, ub, wp, mloc,
    xh, yh, dh, cx, cy_, cd, sx, sy, rx, ry, rd,
    m1s, m1r, m2s, m2r, m3s, m3r, m4s, m4r,
    hs_sem, hr_sem, es_sem, er_sem, s1, r1, s2, r2, s3, r3, s4, r4, osem,
):
    p = lax.axis_index("dx")
    q = lax.axis_index("dy")
    ndx, ndy = ZL * NYC, ZH * NXC * CORES
    zl, yc = p // NYC, p % NYC
    core, xc, zh = q % CORES, (q // CORES) % NXC, q // (CORES * NXC)
    pm, pp = (p + ndx - 1) % ndx, (p + 1) % ndx
    qm, qp = (q + ndy - 1) % ndy, (q + 1) % ndy

    def dy_of(zhv, xv, cv):
        return (zhv * NXC + xv) * CORES + cv

    neighbours = [(pm, q), (pp, q), (p, qm), (p, qp), (pm, qm), (pp, qp), (pm, qp), (pp, qm)]
    partner = [(p, dy_of(zh, xc, CORES - 1 - core))]
    row = [(p, dy_of(zh, (xc + k) % NXC, core)) for k in range(1, NXC)]
    nz = ZL * ZH
    zi = zh * ZL + zl
    column = []
    for k in range(1, nz):
        other = (zi + k) % nz
        column.append(((other % ZL) * NYC + yc, dy_of(other // ZL, xc, core)))
    group = [((p + k) % ndx, q) for k in range(1, ndx)]

    barrier = pltpu.get_barrier_semaphore()
    greeted = neighbours + partner + row + column + group
    for device in greeted:
        pl.semaphore_signal(barrier, inc=1, device_id=device, device_id_type=MESH)
    pl.semaphore_wait(barrier, len(greeted))

    def remote(src, dst, ssem, rsem, device):
        return pltpu.make_async_remote_copy(
            src_ref=src, dst_ref=dst, send_sem=ssem, recv_sem=rsem, device_id=device, device_id_type=MESH
        )

    halo = [
        remote(vec.at[:, 0], xh, hs_sem.at[0], hr_sem.at[0], (pm, q)),
        remote(vec.at[:, :, 0], yh, hs_sem.at[1], hr_sem.at[1], (p, qm)),
        remote(vec.at[:, 0, 0], dh, hs_sem.at[2], hr_sem.at[2], (pm, qm)),
        remote(coef.at[0], cx, hs_sem.at[3], hr_sem.at[3], (pm, q)),
        remote(coef.at[LO], cy_, hs_sem.at[4], hr_sem.at[4], (p, qm)),
        remote(coef.at[0], cd, hs_sem.at[5], hr_sem.at[5], (pm, qm)),
    ]
    for copy in halo:
        copy.start()

    def spread(tile, lane):
        return jnp.broadcast_to(tile[:, lane : lane + 1], (EZ, W))

    def coefs(i, j, mass, pot):
        im[i, j] = mass
        bt[i, j] = (pot - center_shift) * (1.0 / half_width)

    def begin(i, j, values):
        for b in range(BLOCKS):
            value = values[b].astype(F32)
            y[0, b, i, j] = value
            uf[b, i, j] = value * im[i, j]

    def fill(i, carry):
        tile = coef[i]
        for j in range(EZ):
            coefs(i, j, spread(tile, j), spread(tile, EZ + j))
        for b in range(BLOCKS):
            value = vec[b, i].astype(F32)
            y[0, b, i, 0:16] = value
            uf[b, i, 0:16] = value * im[i, 0:16]
        return carry

    lax.fori_loop(0, LO, fill, 0)
    y[1] = jnp.zeros_like(y[1])

    def permute(c, carry):
        place = pos[c]
        onehot = (lax.broadcasted_iota(jnp.int32, (KP, KP), 0) == place).astype(F32).astype(BF16)
        rows = jnp.dot(onehot, amat[...], preferred_element_type=F32).astype(BF16)
        ac[c] = lax.dot_general(rows, onehot, (((1,), (1,)), ((), ())), preferred_element_type=F32).astype(BF16)
        return carry

    lax.fori_loop(0, NCELL, permute, 0)

    for copy in halo:
        copy.wait()
    tile = cx[...]
    for j in range(EZ):
        coefs(LO, j, spread(tile, j), spread(tile, EZ + j))
    tile = cy_[...]
    for i in range(LO):
        coefs(i, 16, spread(tile, i), spread(tile, LO + i))
    tile = cd[...]
    coefs(LO, 16, spread(tile, 0), spread(tile, EZ))
    for b in range(BLOCKS):
        value = xh[b].astype(F32)
        y[0, b, LO, 0:16] = value
        uf[b, LO, 0:16] = value * im[LO, 0:16]
        value = yh[b].astype(F32)
        y[0, b, 0:LO, 16] = value
        uf[b, 0:LO, 16] = value * im[0:LO, 16]
        value = dh[b].astype(F32)
        y[0, b, LO, 16] = value
        uf[b, LO, 16] = value * im[LO, 16]

    def exchange(d):
        plan = [
            (sx.at[d, 0], rx.at[d, 1], (pm, q)),
            (sx.at[d, 1], rx.at[d, 0], (pp, q)),
            (sy.at[d, 0], ry.at[d, 1], (p, qm)),
            (sy.at[d, 1], ry.at[d, 0], (p, qp)),
            (sx.at[d, 0, :, 0], rd.at[d, 3], (pm, qm)),
            (sx.at[d, 1, :, 16], rd.at[d, 0], (pp, qp)),
            (sx.at[d, 0, :, 16], rd.at[d, 2], (pm, qp)),
            (sx.at[d, 1, :, 0], rd.at[d, 1], (pp, qm)),
        ]
        return [remote(s, t, es_sem.at[d, n], er_sem.at[d, n], to) for n, (s, t, to) in enumerate(plan)]

    def apply(d, carry):
        now, later = lax.rem(d, 2), lax.rem(d + 1, 2)
        scale = jnp.where(d == 0, 1.0, 2.0).astype(F32)
        keep = jnp.where(d == 0, 0.0, 1.0).astype(F32)
        for cy in range(2):
            for cz in range(2):
                c = cy * 2 + cz
                kp = (8 * cz + 8) % 16
                for b in range(BLOCKS):
                    flat = uf.at[b].reshape(EX * EY * EZ, W)
                    main = uf[b, :, 8 * cy : 8 * cy + 9, 8 * cz : 8 * cz + 8, :].reshape(648, W)
                    planes = [flat[pl.ds((i * EY + 8 * cy) * EZ + kp, 8, EZ), :] for i in range(EX)]
                    start = (8 * cy + 8) * EZ + kp
                    line = flat[pl.ds(start, 8, EY * EZ), :]
                    last = flat[pl.ds(start + 8 * EY * EZ, 1), :]
                    first = lax.broadcasted_iota(jnp.int32, (8, W), 0) == 0
                    last = jnp.where(first, jnp.broadcast_to(last, (8, W)), 0.0)
                    whole = jnp.concatenate([main] + planes + [line, last, jnp.zeros((32, W), F32)], axis=0)
                    ub[:, b * W : (b + 1) * W] = whole.astype(BF16)
                w = jnp.dot(ac[c], ub[...], preferred_element_type=F32)
                wp[c] = w[648:]
                for b in range(BLOCKS):
                    block = w[:648, b * W : (b + 1) * W].reshape(EX, 9, 8, W)
                    ks = slice(8 * cz, 8 * cz + 8)
                    if cy == 0:
                        acc[b, :, 0:9, ks, :] = block
                    else:
                        acc[b, :, 8, ks, :] += block[:, 0]
                        acc[b, :, 9:17, ks, :] = block[:, 1:]
        for cy in range(2):
            for cz in range(2):
                c = cy * 2 + cz
                kp = (8 * cz + 8) % 16
                for b in range(BLOCKS):
                    flat = acc.at[b].reshape(EX * EY * EZ, W)
                    cols = slice(b * W, (b + 1) * W)
                    for i in range(EX):
                        where = pl.ds((i * EY + 8 * cy) * EZ + kp, 8, EZ)
                        flat[where, :] = flat[where, :] + wp[c, 8 * i : 8 * i + 8, cols]
                    start = (8 * cy + 8) * EZ + kp
                    where = pl.ds(start, 8, EY * EZ)
                    flat[where, :] = flat[where, :] + wp[c, 72:80, cols]
                    where = pl.ds(start + 8 * EY * EZ, 1)
                    flat[where, :] = flat[where, :] + wp[c, 80:81, cols]
        for b in range(BLOCKS):
            sx[d, 0, b] = acc[b, 0].astype(BF16)
            sx[d, 1, b] = acc[b, LO].astype(BF16)
            sy[d, 0, b] = acc[b, :, 0].astype(BF16)
            sy[d, 1, b] = acc[b, :, 16].astype(BF16)
        copies = exchange(d)
        for copy in copies:
            copy.start()

        def update(b, i, j):
            mass = im[i, j]
            fresh = scale * (acc[b, i, j] * (mass * (1.0 / half_width)) + bt[i, j] * y[now, b, i, j]) - keep * y[later, b, i, j]
            y[later, b, i, j] = fresh
            uf[b, i, j] = fresh * mass

        def inner(i, carry):
            for b in range(BLOCKS):
                update(b, i, slice(1, 16))
            return carry

        lax.fori_loop(1, LO, inner, 0)
        for copy in copies:
            copy.wait()
        for b in range(BLOCKS):
            acc[b, 0] += rx[d, 0, b].astype(F32)
            acc[b, LO] += rx[d, 1, b].astype(F32)
            acc[b, :, 0] += ry[d, 0, b].astype(F32)
            acc[b, :, 16] += ry[d, 1, b].astype(F32)
            acc[b, 0, 0] += rd[d, 0, b].astype(F32)
            acc[b, 0, 16] += rd[d, 1, b].astype(F32)
            acc[b, LO, 0] += rd[d, 2, b].astype(F32)
            acc[b, LO, 16] += rd[d, 3, b].astype(F32)
        for b in range(BLOCKS):
            update(b, 0, slice(0, 17))
            update(b, LO, slice(0, 17))
            update(b, slice(1, LO), 0)
            update(b, slice(1, LO), 16)
        return carry

    lax.fori_loop(0, DEGREE, apply, 0)
    final = DEGREE % 2
    writes = [
        pltpu.make_async_copy(y.at[final, b, pl.ds(0, LO), pl.ds(0, 16)], out.at[b], osem.at[b])
        for b in range(BLOCKS)
    ]
    for copy in writes:
        copy.start()

    mloc[...] = jnp.zeros_like(mloc)

    def product(i, carry):
        cols = [y[final, b, i, 0:16].reshape(256, W).astype(BF16) for b in range(BLOCKS)]
        right = jnp.concatenate(cols, axis=1)
        left = res[i]
        mloc[...] += lax.dot_general(left, right, (((0,), (0,)), ((), ())), preferred_element_type=F32)
        return carry

    lax.fori_loop(0, LO, product, 0)

    span = CORES * 16
    for g in range(ZH * NXC):
        m1s[g] = (mloc[pl.ds(pl.multiple_of(g * span + (CORES - 1 - core) * 16, 16), 16), :] * norm_scale).astype(BF16)
    copy = remote(m1s, m1r, s1.at[0], r1.at[0], partner[0])
    copy.start()
    copy.wait()

    def both(g):
        own = mloc[pl.ds(pl.multiple_of(g * span + core * 16, 16), 16), :] * norm_scale
        return own + m1r[g].astype(F32)

    for zv in range(ZH):
        for k in range(1, NXC):
            m2s[k - 1, zv] = both(zv * NXC + (xc + k) % NXC).astype(BF16)
    copies = [remote(m2s.at[k], m2r.at[k], s2.at[k], r2.at[k], row[k]) for k in range(NXC - 1)]
    for copy in copies:
        copy.start()
    for copy in copies:
        copy.wait()
    for zv in range(ZH):
        total = both(zv * NXC + xc)
        for k in range(NXC - 1):
            total = total + m2r[k, zv].astype(F32)
        for half in range(ZL):
            m3s[zv * ZL + half] = total[half * 8 : half * 8 + 8]
    copies = [
        remote(m3s.at[(zi + k + 1) % nz], m3r.at[k], s3.at[k], r3.at[k], column[k]) for k in range(nz - 1)
    ]
    for copy in copies:
        copy.start()
    for copy in copies:
        copy.wait()
    total = m3s[zi]
    for k in range(nz - 1):
        total = total + m3r[k]
    m4s[...] = total
    m4r[p] = total
    copies = [remote(m4s, m4r.at[p], s4.at[k], r4.at[k], group[k]) for k in range(ndx - 1)]
    for copy in copies:
        copy.start()
    for copy in copies:
        copy.wait()
    for half in range(ZL):
        total = m4r[half * NYC]
        for k in range(1, NYC):
            total = total + m4r[half * NYC + k]
        margin[half * 8 : half * 8 + 8, :] = total
    for copy in writes:
        copy.wait()


def places(connectivity):
    index = connectivity.reshape(NCELL, -1)
    cell = jnp.arange(NCELL, dtype=jnp.int32)[:, None]
    cy, cz = cell // 2, cell % 2
    i = index // (EY * EZ)
    j = index // EZ % EY - 8 * cy
    k = index % EZ
    inside = k // 8 == cz
    plane = jnp.where(j < 8, 648 + i * 8 + j, 720 + i)
    where = jnp.where(inside, (i * 9 + j) * 8 + k % 8, plane)
    where = jnp.pad(where, ((0, 0), (0, KP - where.shape[1])), constant_values=-1)
    return where.reshape(NCELL, 1, KP)


def body(vectors, resident, inv_mass, potential, cell_matrix, connectivity):
    total_nodes = inv_mass.size * lax.axis_size("dx") * lax.axis_size("dy")
    norm_scale = 1.0 / math.sqrt(total_nodes)
    pos = places(connectivity)
    nc = cell_matrix.shape[0]
    amat = jnp.pad(cell_matrix, ((0, KP - nc), (0, KP - nc)))
    both = jnp.concatenate([inv_mass.transpose(0, 2, 1), potential.transpose(0, 2, 1)], axis=-1)
    edge = jnp.concatenate([inv_mass[:, 0].T, potential[:, 0].T], axis=-1)
    coef = jnp.concatenate(
        [jnp.pad(both, ((0, 0), (0, 0), (0, W - 32))), jnp.pad(edge, ((0, 0), (0, W - 16)))[None]], axis=0
    )
    res = resident.reshape(LO, 256, resident.shape[-1])
    ndx, ndy = ZL * NYC, ZH * NXC * CORES
    nz = ZL * ZH
    rows = 16 * ndy
    vmem = pl.BlockSpec(memory_space=pltpu.VMEM)
    dma = pltpu.SemaphoreType.DMA

    def k(*refs):
        kernel(norm_scale, *refs)

    state = (BLOCKS, EX, EY, EZ, W)
    return pl.pallas_call(
        k,
        out_shape=(
            jax.ShapeDtypeStruct((BLOCKS, LO, 16, EZ, W), F32),
            jax.ShapeDtypeStruct((16, BLOCKS * W), F32),
        ),
        in_specs=[vmem] * 5,
        out_specs=(pl.BlockSpec(memory_space=pl.ANY), vmem),
        scratch_shapes=[
            pltpu.VMEM((NCELL, KP, KP), BF16),
            pltpu.VMEM(state, F32),
            pltpu.VMEM(state, F32),
            pltpu.VMEM((2, *state), F32),
            pltpu.VMEM((EX, EY, EZ, W), F32),
            pltpu.VMEM((EX, EY, EZ, W), F32),
            pltpu.VMEM((KP, BLOCKS * W), BF16),
            pltpu.VMEM((NCELL, KP - 648, BLOCKS * W), F32),
            pltpu.VMEM((rows, BLOCKS * W), F32),
            pltpu.VMEM((BLOCKS, 16, EZ, W), BF16),
            pltpu.VMEM((BLOCKS, LO, EZ, W), BF16),
            pltpu.VMEM((BLOCKS, EZ, W), BF16),
            pltpu.VMEM((EZ, W), F32),
            pltpu.VMEM((EZ, W), F32),
            pltpu.VMEM((EZ, W), F32),
            pltpu.VMEM((DEGREE, 2, BLOCKS, EY, EZ, W), BF16),
            pltpu.VMEM((DEGREE, 2, BLOCKS, EX, EZ, W), BF16),
            pltpu.VMEM((DEGREE, 2, BLOCKS, EY, EZ, W), BF16),
            pltpu.VMEM((DEGREE, 2, BLOCKS, EX, EZ, W), BF16),
            pltpu.VMEM((DEGREE, 4, BLOCKS, EZ, W), BF16),
            pltpu.VMEM((ZH * NXC, 16, BLOCKS * W), BF16),
            pltpu.VMEM((ZH * NXC, 16, BLOCKS * W), BF16),
            pltpu.VMEM((NXC - 1, ZH, 16, BLOCKS * W), BF16),
            pltpu.VMEM((NXC - 1, ZH, 16, BLOCKS * W), BF16),
            pltpu.VMEM((nz, 8, BLOCKS * W), F32),
            pltpu.VMEM((nz - 1, 8, BLOCKS * W), F32),
            pltpu.VMEM((8, BLOCKS * W), F32),
            pltpu.VMEM((ndx, 8, BLOCKS * W), F32),
            dma((6,)), dma((6,)), dma((DEGREE, 8)), dma((DEGREE, 8)),
            dma((1,)), dma((1,)), dma((NXC - 1,)), dma((NXC - 1,)),
            dma((nz - 1,)), dma((nz - 1,)), dma((ndx - 1,)), dma((ndx - 1,)), dma((BLOCKS,)),
        ],
        compiler_params=pltpu.CompilerParams(
            collective_id=0, has_side_effects=True, vmem_limit_bytes=60 * 1024 * 1024
        ),
    )(vectors, res, coef, pos, amat)


def solution(mesh):
    return jax.shard_map(
        body,
        mesh=mesh,
        in_specs=(
            P(None, "dx", "dy", None, None),
            P("dx", "dy", None, None),
            P("dx", "dy", None),
            P("dx", "dy", None),
            P(),
            P("dx", "dy", None, None),
        ),
        out_specs=(P(None, "dx", "dy", None, None), P("dy", None)),
        check_vma=False,
    )
```

time: 265 us -> 83.5 us (0.32); the launches traced: 262 us -> 83.1 us
  other arithmetic: 74.4 us -> 1.6 us
  Pallas kernels: 0 us -> 70.6 us
  local copies, waits for them, and re-layouts: 65.4 us -> 10.2 us
  waiting for transfers between devices: 49.8 us -> 0 us
  blocking collectives: 34 us -> 0 us
  starting transfers between devices: 23 us -> 0 us
  matrix products: 13.8 us -> 0 us
    pallas_call x0 -> x1, Pallas kernels: none -> 70.6 us  [body(): pl.pallas_call(k, out_shape=(jax.ShapeDtypeStruct((BLOCKS, LO, 16, EZ, W)...]
    scatter-add x9 -> x0, other arithmetic: 55.3 us -> none  [the longest x3 52.4 us: apply_hamiltonian(): jax.ops.segment_sum(product.reshape(-1, vec_width), node_index, num_segme...]
    ppermute x12 -> x0, waiting for transfers between devices: 46.5 us -> none  [from_behind(): return lax.ppermute(value, axis, pairs)]
    all_to_all x1 -> x0, blocking collectives: 34 us -> none  [sum_at_owner(): lax.all_to_all(cut_along(value, dim, length), axis, 0, 0, tiled=True)]
    gather x3 -> x0, local copies, waits for them, and re-layouts: 28.9 us -> none  [apply_hamiltonian(): jnp.take(grown.reshape(-1, vec_width), node_index, axis=0)]
    reshape x6 -> x1, local copies, waits for them, and re-layouts: 20.8 us -> 0.61 us  [places(): return where.reshape(NCELL, 1, KP)]
    ppermute x12 -> x0, starting transfers between devices: 19.6 us -> none  [from_behind(): return lax.ppermute(value, axis, pairs)]
    dot_general x4 -> x0, matrix products: 13.8 us -> none  [the longest x3 13.1 us: apply_hamiltonian(): jnp.einsum('il,clw->ciw', cell_matrix, picked, preferred_element_type=jnp...]
  transfers between devices with their start and end apart: 13 -> 0, of which waited for: 12 -> 0; matrix products, arithmetic and copies ran while one was open for 4% -> 0% of each run, Pallas kernels for 0% -> 0%
where the time goes in v1:
time: 83.5 us; the launch traced here: 83.1 us
  Pallas kernels  70.6 us (85%)
  local copies, waits for them, and re-layouts  10.2 us (12%)
  other arithmetic  1.6 us (2%)
    pallas_call x1, Pallas kernels, body(): pl.pallas_call(k, out_shape=(jax.ShapeDtypeStruct((BLOCKS, LO, 16, EZ, W)...  70.6 us
    unnamed x6, local copies, waits for them, and re-layouts  5.54 us
    pad x1, local copies, waits for them, and re-layouts, body(): amat = jnp.pad(cell_matrix, ((0, KP - nc), (0, KP - nc)))  2.37 us

profile of v1, /device:TPU:4, one launch (start us, length us, event | category | flops | bytes accessed | tf_op | source)
XLA Modules:
  0.0 83.1 jit_solution(7037257710604227134)
XLA Ops:
  0.6 0.8 slice.6
  1.4 0.1 copy.11
  1.5 0.8 slice.7
  2.2 0.1 copy.13
  2.3 0.1 fusion.11
  2.4 0.8 fusion.4
  3.2 0.6 reshape.69.refs_3_
  3.8 0.9 %copy.8 = f32[8,16,16]{1,2,0:T(8,128)S(1)} copy(f32[8,16,16]{2,1,0:T(8,128)} %param.8) | data formatting | bytes 16384 | tf_op args[2]
  4.7 0.9 %copy.9 = f32[8,16,16]{1,2,0:T(8,128)S(1)} copy(f32[8,16,16]{2,1,0:T(8,128)} %param.9) | data formatting | bytes 16384 | tf_op args[3]
  5.6 0.1 select_maximum_fusion
  5.7 0.6 pad_maximum_fusion.refs_2_
  6.4 2.4 %pad.19.refs_4_ = bf16[768,768]{1,0:T(8,128)(2,1)} pad(bf16[729,729]{1,0:T(8,128)(2,1)} %param.10, bf16[]{:T(256)} %constant.101.clone.1), padding=0_39x0_39 | pad | bytes 2242532 | tf_op jit(solution)/shard_map/jit(_pad)/pad | solution.py:317
  8.8 70.6 %shard_map.77 = (f32[2,8,16,16,128]{4,3,2,1,0:T(8,128)}, f32[16,256]{1,0:T(8,128)}) custom-call(bf16[2,8,16,16,128]{4,3,2,1,0:T(8,128)(2,1)} %refs_0_.1, bf16[8,256,512]{2,1,0:T(8,128)(2,1)} %bitcast.37, f32[9,16,128]{2,1,0:T(8,128)} %pad_maximum_fusion.refs_2_, s32[4,1,768]{2,1,0:T(1,128)} %reshape.69.refs_3_, bf16[768,768]{1,0:T(8,128)(2,1)} %pad.19.refs_4_), custom_call_target="tpu_custom_call" | custom-call | tf_op jit(solution)/shard_map/pallas_call | solution.py:334
  79.4 0.0 copy-start
  79.4 3.1 %copy.18 = f32[2,8,16,16,128]{4,3,2,1,0:T(8,128)} copy(f32[2,8,16,16,128]{4,3,2,1,0:T(8,128)} %get-tuple-element.6) | data formatting | bytes 4194304
  82.5 0.0 copy-done
  82.5 0.6 copy.19
  (2 shorter events, 0.0 us)
Async XLA Ops:
  79.4 3.1 %copy-start = (f32[16,256]{1,0:T(8,128)S(1)}, f32[16,256]{1,0:T(8,128)}, u32[]{:S(2)}) copy-start(f32[16,256]{1,0:T(8,128)} %get-tuple-element.7) | copy-start | bytes 49156

commit v2 on v1

v2 whole, which is shorter than its diff:
```python
import math

import jax
import jax.numpy as jnp
from jax import lax
from jax.experimental import pallas as pl
from jax.experimental.pallas import tpu as pltpu
from jax.sharding import PartitionSpec as P

MESH = pl.DeviceIdType.MESH
BLOCKS = 2
DEGREE = 3
NCELL = 4
KP = 768
LO, EX, EY, EZ = 8, 9, 17, 16
W = 128
center_shift = 1.2
half_width = 2.0
ZL, NYC = 2, 4
ZH, NXC, CORES = 4, 4, 2
F32, BF16 = jnp.float32, jnp.bfloat16


def kernel(
    norm_scale, vec, res, mass, pot, amat, conn, out, margin,
    ap, ac, acc, uf, y, im, bt, ub, wp, mloc, rs, posr, ct,
    xh, yh, dh, cx, cy_, cd, sx, sy, rx, ry, rd,
    m1s, m1r, m2s, m2r, m3s, m3r, m4s, m4r,
    hs_sem, hr_sem, es_sem, er_sem, s1, r1, s2, r2, s3, r3, s4, r4, osem, lsem,
):
    p = lax.axis_index("dx")
    q = lax.axis_index("dy")
    ndx, ndy = ZL * NYC, ZH * NXC * CORES
    zl, yc = p // NYC, p % NYC
    core, xc, zh = q % CORES, (q // CORES) % NXC, q // (CORES * NXC)
    pm, pp = (p + ndx - 1) % ndx, (p + 1) % ndx
    qm, qp = (q + ndy - 1) % ndy, (q + 1) % ndy

    def dy_of(zhv, xv, cv):
        return (zhv * NXC + xv) * CORES + cv

    neighbours = [(pm, q), (pp, q), (p, qm), (p, qp), (pm, qm), (pp, qp), (pm, qp), (pp, qm)]
    partner = [(p, dy_of(zh, xc, CORES - 1 - core))]
    row = [(p, dy_of(zh, (xc + k) % NXC, core)) for k in range(1, NXC)]
    nz = ZL * ZH
    zi = zh * ZL + zl
    column = []
    for k in range(1, nz):
        other = (zi + k) % nz
        column.append(((other % ZL) * NYC + yc, dy_of(other // ZL, xc, core)))
    group = [((p + k) % ndx, q) for k in range(1, ndx)]

    barrier = pltpu.get_barrier_semaphore()
    greeted = neighbours + partner + row + column + group
    for device in greeted:
        pl.semaphore_signal(barrier, inc=1, device_id=device, device_id_type=MESH)
    load = pltpu.make_async_copy(res, rs.at[pl.ds(0, LO), pl.ds(0, 16)], lsem.at[0])
    load.start()

    def remote(src, dst, ssem, rsem, device):
        return pltpu.make_async_remote_copy(
            src_ref=src, dst_ref=dst, send_sem=ssem, recv_sem=rsem, device_id=device, device_id_type=MESH
        )

    ct[0] = mass[...].reshape(LO * 16, EZ).T
    ct[1] = pot[...].reshape(LO * 16, EZ).T

    index = conn[0, 0]
    cell = lax.broadcasted_iota(jnp.int32, index.shape, 0)
    k = index & 15
    t = index >> 4
    i = (t * 241) >> 12
    j = t - i * EY - 8 * (cell >> 1)
    inside = (k >> 3) == (cell & 1)
    plane = jnp.where(j < 8, 648 + i * 8 + j, 720 + i)
    where = jnp.where(inside, (i * 9 + j) * 8 + (k & 7), plane)
    posr[...] = jnp.full(posr.shape, -1, jnp.int32)
    nc = index.shape[1]
    for c in range(NCELL):
        posr[c, :, 0:nc] = where[c : c + 1]
    ap[...] = jnp.zeros_like(ap)
    ap[0:nc, 0:nc] = amat[...]

    def spread(tile, lane):
        return jnp.broadcast_to(tile[:, lane : lane + 1], (EZ, W))

    def coefs(i, j, mass_ij, pot_ij):
        im[i, j] = mass_ij
        bt[i, j] = (pot_ij - center_shift) * (1.0 / half_width)

    for i in range(LO):
        for j in range(16):
            coefs(i, j, spread(ct[0], i * 16 + j), spread(ct[1], i * 16 + j))

    def permute(c, carry):
        onehot = (lax.broadcasted_iota(jnp.int32, (KP, KP), 0) == posr[c]).astype(F32).astype(BF16)
        rows = jnp.dot(onehot, ap[...], preferred_element_type=F32).astype(BF16)
        ac[c] = lax.dot_general(rows, onehot, (((1,), (1,)), ((), ())), preferred_element_type=F32).astype(BF16)
        return carry

    lax.fori_loop(0, 1, permute, 0)

    pl.semaphore_wait(barrier, len(greeted))
    halo = [
        remote(ct, cd, hs_sem.at[5], hr_sem.at[5], (pm, qm)),
        remote(vec.at[:, 0, 0], dh, hs_sem.at[2], hr_sem.at[2], (pm, qm)),
        remote(ct, cx, hs_sem.at[3], hr_sem.at[3], (pm, q)),
        remote(ct, cy_, hs_sem.at[4], hr_sem.at[4], (p, qm)),
        remote(vec.at[:, 0], xh, hs_sem.at[0], hr_sem.at[0], (pm, q)),
        remote(vec.at[:, :, 0], yh, hs_sem.at[1], hr_sem.at[1], (p, qm)),
    ]
    for copy in halo:
        copy.start()
    rhalo = [
        remote(res.at[0], rs.at[LO, pl.ds(0, 16)], hs_sem.at[6], hr_sem.at[6], (pm, q)),
        remote(res.at[:, 0], rs.at[pl.ds(0, LO), 16], hs_sem.at[7], hr_sem.at[7], (p, qm)),
        remote(res.at[0, 0], rs.at[LO, 16], hs_sem.at[8], hr_sem.at[8], (pm, qm)),
    ]
    for copy in rhalo:
        copy.start()

    def fill(i, carry):
        for b in range(BLOCKS):
            value = vec[b, i].astype(F32)
            y[0, b, i, 0:16] = value
            uf[b, i, 0:16] = value * im[i, 0:16]
        return carry

    lax.fori_loop(0, LO, fill, 0)
    y[1] = jnp.zeros_like(y[1])
    lax.fori_loop(1, NCELL, permute, 0)

    for copy in halo:
        copy.wait()
    for j in range(16):
        coefs(LO, j, spread(cx[0], j), spread(cx[1], j))
    for i in range(LO):
        coefs(i, 16, spread(cy_[0], i * 16), spread(cy_[1], i * 16))
    coefs(LO, 16, spread(cd[0], 0), spread(cd[1], 0))
    for b in range(BLOCKS):
        value = xh[b].astype(F32)
        y[0, b, LO, 0:16] = value
        uf[b, LO, 0:16] = value * im[LO, 0:16]
        value = yh[b].astype(F32)
        y[0, b, 0:LO, 16] = value
        uf[b, 0:LO, 16] = value * im[0:LO, 16]
        value = dh[b].astype(F32)
        y[0, b, LO, 16] = value
        uf[b, LO, 16] = value * im[LO, 16]

    low, high = pl.ds(0, 8), pl.ds(8, 9)

    def exchange(d, part):
        if part == 0:
            plan = [
                (0, sx.at[d, 0, :, low], rx.at[d, 1, :, low], (pm, q)),
                (1, sx.at[d, 1, :, low], rx.at[d, 0, :, low], (pp, q)),
                (2, sy.at[d, 0], ry.at[d, 1], (p, qm)),
                (4, sx.at[d, 0, :, 0], rd.at[d, 3], (pm, qm)),
                (7, sx.at[d, 1, :, 0], rd.at[d, 1], (pp, qm)),
            ]
            wanted = (1,)
        else:
            plan = [
                (8, sx.at[d, 0, :, high], rx.at[d, 1, :, high], (pm, q)),
                (9, sx.at[d, 1, :, high], rx.at[d, 0, :, high], (pp, q)),
                (3, sy.at[d, 1], ry.at[d, 0], (p, qp)),
                (5, sx.at[d, 1, :, 16], rd.at[d, 0], (pp, qp)),
                (6, sx.at[d, 0, :, 16], rd.at[d, 2], (pm, qp)),
            ]
            wanted = (9, 3, 5)
        last = isinstance(d, int) and d == DEGREE - 1
        return [
            remote(s, t, es_sem.at[d, n], er_sem.at[d, n], to) for n, s, t, to in plan if n in wanted or not last
        ]

    def cells(d, cy):
        for cz in range(2):
            c = cy * 2 + cz
            kp = (8 * cz + 8) % 16
            for b in range(BLOCKS):
                flat = uf.at[b].reshape(EX * EY * EZ, W)
                main = uf[b, :, 8 * cy : 8 * cy + 9, 8 * cz : 8 * cz + 8, :].reshape(648, W)
                planes = [flat[pl.ds((i * EY + 8 * cy) * EZ + kp, 8, EZ), :] for i in range(EX)]
                start = (8 * cy + 8) * EZ + kp
                line = flat[pl.ds(start, 8, EY * EZ), :]
                last = flat[pl.ds(start + 8 * EY * EZ, 1), :]
                first = lax.broadcasted_iota(jnp.int32, (8, W), 0) == 0
                last = jnp.where(first, jnp.broadcast_to(last, (8, W)), 0.0)
                whole = jnp.concatenate([main] + planes + [line, last, jnp.zeros((32, W), F32)], axis=0)
                ub[c, :, b * W : (b + 1) * W] = whole.astype(BF16)
            w = jnp.dot(ac[c], ub[c], preferred_element_type=F32)
            wp[c] = w[648:]
            for b in range(BLOCKS):
                block = w[:648, b * W : (b + 1) * W].reshape(EX, 9, 8, W)
                ks = slice(8 * cz, 8 * cz + 8)
                if cy == 0:
                    acc[b, :, 0:9, ks, :] = block
                else:
                    acc[b, :, 8, ks, :] += block[:, 0]
                    acc[b, :, 9:17, ks, :] = block[:, 1:]
        for cz in range(2):
            c = cy * 2 + cz
            kp = (8 * cz + 8) % 16
            for b in range(BLOCKS):
                flat = acc.at[b].reshape(EX * EY * EZ, W)
                cols = slice(b * W, (b + 1) * W)
                for i in range(EX):
                    where = pl.ds((i * EY + 8 * cy) * EZ + kp, 8, EZ)
                    flat[where, :] = flat[where, :] + wp[c, 8 * i : 8 * i + 8, cols]
                start = (8 * cy + 8) * EZ + kp
                where = pl.ds(start, 8, EY * EZ)
                flat[where, :] = flat[where, :] + wp[c, 72:80, cols]
                where = pl.ds(start + 8 * EY * EZ, 1)
                flat[where, :] = flat[where, :] + wp[c, 80:81, cols]
        js = slice(0, 8) if cy == 0 else slice(8, 17)
        for b in range(BLOCKS):
            sx[d, 0, b, js] = acc[b, 0, js].astype(BF16)
            sx[d, 1, b, js] = acc[b, LO, js].astype(BF16)
            sy[d, cy, b] = acc[b, :, 16 * cy].astype(BF16)
        copies = exchange(d, cy)
        for copy in copies:
            copy.start()
        return copies

    def apply(d, now, later, scale, keep, close):
        copies = cells(d, 0) + cells(d, 1)

        def inner(i, carry):
            for b in range(BLOCKS):
                m = im[i]
                fresh = scale * (acc[b, i] * (m * (1.0 / half_width)) + bt[i] * y[now, b, i]) - keep * y[later, b, i]
                y[later, b, i] = fresh
                uf[b, i] = fresh * m
            return carry

        lax.fori_loop(0, EX, inner, 0)

        def add(b, i, j, part):
            y[later, b, i, j] = y[later, b, i, j] + (scale * (1.0 / half_width)) * im[i, j] * part.astype(F32)

        def refresh(b, i, j):
            uf[b, i, j] = y[later, b, i, j] * im[i, j]

        def arrive():
            for copy in copies:
                copy.wait()
            for b in range(BLOCKS):
                add(b, 0, slice(0, 17), rx[d, 0, b])
                add(b, slice(0, EX), 0, ry[d, 0, b])
                add(b, 0, 0, rd[d, 0, b])
                add(b, LO, slice(0, 17), rx[d, 1, b])
                add(b, slice(0, EX), 16, ry[d, 1, b])
                add(b, 0, 16, rd[d, 1, b])
                add(b, LO, 0, rd[d, 2, b])
                add(b, LO, 16, rd[d, 3, b])
                refresh(b, 0, slice(0, 17))
                refresh(b, LO, slice(0, 17))
                refresh(b, slice(1, LO), 0)
                refresh(b, slice(1, LO), 16)

        def arrive_last():
            for copy in copies:
                copy.wait()
            for b in range(BLOCKS):
                add(b, 0, slice(0, 16), rx[d, 0, b, 0:16])
                add(b, slice(0, LO), 0, ry[d, 0, b, 0:LO])
                add(b, 0, 0, rd[d, 0, b])

        if close:
            arrive()
            return None
        return arrive_last

    def step(d, carry):
        scale = jnp.where(d == 0, 1.0, 2.0).astype(F32)
        keep = jnp.where(d == 0, 0.0, 1.0).astype(F32)
        apply(d, lax.rem(d, 2), lax.rem(d + 1, 2), scale, keep, True)
        return carry

    lax.fori_loop(0, DEGREE - 1, step, 0)
    final = DEGREE % 2
    y[1 - final, :, LO] = jnp.zeros((BLOCKS, EY, EZ, W), F32)
    y[final, :, LO] = jnp.zeros((BLOCKS, EY, EZ, W), F32)
    y[1 - final, :, 0:LO, 16] = jnp.zeros((BLOCKS, LO, EZ, W), F32)
    y[final, :, 0:LO, 16] = jnp.zeros((BLOCKS, LO, EZ, W), F32)
    arrive_last = apply(DEGREE - 1, 1 - final, final, 2.0, 1.0, False)

    load.wait()
    for copy in rhalo:
        copy.wait()
    nres = rs.shape[-1]
    right = jnp.concatenate([y[final, b, :, 16].reshape(EX * EZ, W).astype(BF16) for b in range(BLOCKS)], axis=1)
    mloc[...] = lax.dot_general(
        rs[:, 16].reshape(EX * EZ, nres), right, (((0,), (0,)), ((), ())), preferred_element_type=F32
    )

    def product(i, carry):
        cols = [y[final, b, i, 0:16].reshape(256, W).astype(BF16) for b in range(BLOCKS)]
        right = jnp.concatenate(cols, axis=1)
        left = rs[i, 0:16].reshape(256, nres)
        mloc[...] += lax.dot_general(left, right, (((0,), (0,)), ((), ())), preferred_element_type=F32)
        return carry

    lax.fori_loop(0, EX, product, 0)

    span = CORES * 16
    for g in range(ZH * NXC):
        m1s[g] = (mloc[pl.ds(pl.multiple_of(g * span + (CORES - 1 - core) * 16, 16), 16), :] * norm_scale).astype(BF16)
    copy = remote(m1s, m1r, s1.at[0], r1.at[0], partner[0])
    copy.start()
    copy.wait()

    def both(g):
        own = mloc[pl.ds(pl.multiple_of(g * span + core * 16, 16), 16), :] * norm_scale
        return own + m1r[g].astype(F32)

    for zv in range(ZH):
        for k in range(1, NXC):
            m2s[k - 1, zv] = both(zv * NXC + (xc + k) % NXC).astype(BF16)
    copies = [remote(m2s.at[k], m2r.at[k], s2.at[k], r2.at[k], row[k]) for k in range(NXC - 1)]
    for copy in copies:
        copy.start()
    arrive_last()
    writes = [
        pltpu.make_async_copy(y.at[final, b, pl.ds(0, LO), pl.ds(0, 16)], out.at[b], osem.at[b])
        for b in range(BLOCKS)
    ]
    for copy in writes:
        copy.start()
    for copy in copies:
        copy.wait()
    for zv in range(ZH):
        total = both(zv * NXC + xc)
        for k in range(NXC - 1):
            total = total + m2r[k, zv].astype(F32)
        for half in range(ZL):
            m3s[zv * ZL + half] = total[half * 8 : half * 8 + 8]
    copies = [
        remote(m3s.at[(zi + k + 1) % nz], m3r.at[k], s3.at[k], r3.at[k], column[k]) for k in range(nz - 1)
    ]
    for copy in copies:
        copy.start()
    for copy in copies:
        copy.wait()
    total = m3s[zi]
    for k in range(nz - 1):
        total = total + m3r[k]
    m4s[...] = total
    m4r[p] = total
    copies = [remote(m4s, m4r.at[p], s4.at[k], r4.at[k], group[k]) for k in range(ndx - 1)]
    for copy in copies:
        copy.start()
    for copy in copies:
        copy.wait()
    for half in range(ZL):
        total = m4r[half * NYC]
        for k in range(1, NYC):
            total = total + m4r[half * NYC + k]
        margin[half * 8 : half * 8 + 8, :] = total
    for copy in writes:
        copy.wait()


def body(vectors, resident, inv_mass, potential, cell_matrix, connectivity):
    total_nodes = inv_mass.size * lax.axis_size("dx") * lax.axis_size("dy")
    norm_scale = 1.0 / math.sqrt(total_nodes)
    nres = resident.shape[-1]
    ndx, ndy = ZL * NYC, ZH * NXC * CORES
    nz = ZL * ZH
    rows = 16 * ndy
    vmem = pl.BlockSpec(memory_space=pltpu.VMEM)
    hbm = pl.BlockSpec(memory_space=pl.ANY)
    dma = pltpu.SemaphoreType.DMA

    def k(*refs):
        kernel(norm_scale, *refs)

    state = (BLOCKS, EX, EY, EZ, W)
    return pl.pallas_call(
        k,
        out_shape=(
            jax.ShapeDtypeStruct((BLOCKS, LO, 16, EZ, W), F32),
            jax.ShapeDtypeStruct((16, BLOCKS * W), F32),
        ),
        in_specs=[vmem, hbm, vmem, vmem, vmem, vmem],
        out_specs=(hbm, vmem),
        scratch_shapes=[
            pltpu.VMEM((KP, KP), BF16),
            pltpu.VMEM((NCELL, KP, KP), BF16),
            pltpu.VMEM(state, F32),
            pltpu.VMEM(state, F32),
            pltpu.VMEM((2, *state), F32),
            pltpu.VMEM((EX, EY, EZ, W), F32),
            pltpu.VMEM((EX, EY, EZ, W), F32),
            pltpu.VMEM((NCELL, KP, BLOCKS * W), BF16),
            pltpu.VMEM((NCELL, KP - 648, BLOCKS * W), F32),
            pltpu.VMEM((rows, BLOCKS * W), F32),
            pltpu.VMEM((EX, EY, EZ, nres), BF16),
            pltpu.VMEM((NCELL, 1, KP), jnp.int32),
            pltpu.VMEM((2, EZ, LO * 16), F32),
            pltpu.VMEM((BLOCKS, 16, EZ, W), BF16),
            pltpu.VMEM((BLOCKS, LO, EZ, W), BF16),
            pltpu.VMEM((BLOCKS, EZ, W), BF16),
            pltpu.VMEM((2, EZ, LO * 16), F32),
            pltpu.VMEM((2, EZ, LO * 16), F32),
            pltpu.VMEM((2, EZ, LO * 16), F32),
            pltpu.VMEM((DEGREE, 2, BLOCKS, EY, EZ, W), BF16),
            pltpu.VMEM((DEGREE, 2, BLOCKS, EX, EZ, W), BF16),
            pltpu.VMEM((DEGREE, 2, BLOCKS, EY, EZ, W), BF16),
            pltpu.VMEM((DEGREE, 2, BLOCKS, EX, EZ, W), BF16),
            pltpu.VMEM((DEGREE, 4, BLOCKS, EZ, W), BF16),
            pltpu.VMEM((ZH * NXC, 16, BLOCKS * W), BF16),
            pltpu.VMEM((ZH * NXC, 16, BLOCKS * W), BF16),
            pltpu.VMEM((NXC - 1, ZH, 16, BLOCKS * W), BF16),
            pltpu.VMEM((NXC - 1, ZH, 16, BLOCKS * W), BF16),
            pltpu.VMEM((nz, 8, BLOCKS * W), F32),
            pltpu.VMEM((nz - 1, 8, BLOCKS * W), F32),
            pltpu.VMEM((8, BLOCKS * W), F32),
            pltpu.VMEM((ndx, 8, BLOCKS * W), F32),
            dma((9,)), dma((9,)), dma((DEGREE, 10)), dma((DEGREE, 10)),
            dma((1,)), dma((1,)), dma((NXC - 1,)), dma((NXC - 1,)),
            dma((nz - 1,)), dma((nz - 1,)), dma((ndx - 1,)), dma((ndx - 1,)), dma((BLOCKS,)), dma((1,)),
        ],
        compiler_params=pltpu.CompilerParams(
            collective_id=0, has_side_effects=True, vmem_limit_bytes=44 * 1024 * 1024
        ),
    )(vectors, resident, inv_mass, potential, cell_matrix, connectivity)


def solution(mesh):
    return jax.shard_map(
        body,
        mesh=mesh,
        in_specs=(
            P(None, "dx", "dy", None, None),
            P("dx", "dy", None, None),
            P("dx", "dy", None),
            P("dx", "dy", None),
            P(),
            P("dx", "dy", None, None),
        ),
        out_specs=(P(None, "dx", "dy", None, None), P("dy", None)),
        check_vma=False,
    )
```

time: 83.5 us -> 72.5 us (0.87)
  Pallas kernels: 70.6 us -> 63.2 us
  local copies, waits for them, and re-layouts: 10.2 us -> 8.37 us
  other arithmetic: 1.6 us -> 0 us
    pallas_call x1, Pallas kernels: 70.6 us -> 63.2 us  [body(): pl.pallas_call(k, out_shape=(jax.ShapeDtypeStruct((BLOCKS, LO, 16, EZ, W)...]
    unnamed x6 -> x14, local copies, waits for them, and re-layouts: 5.54 us -> 8.37 us
    pad x2 -> x0, local copies, waits for them, and re-layouts: 2.38 us -> none  [the longest x1 2.37 us: body(): amat = jnp.pad(cell_matrix, ((0, KP - nc), (0, KP - nc)))]
    slice x2 -> x0, local copies, waits for them, and re-layouts: 1.52 us -> none  [body(): edge = jnp.concatenate([inv_mass[:, 0].T, potential[:, 0].T], axis=-1)]
where the time goes in v2:
time: 72.5 us; the launch traced here: 72.2 us
  Pallas kernels  63.2 us (87%)
  local copies, waits for them, and re-layouts  8.37 us (12%)
    pallas_call x1, Pallas kernels, body(): pl.pallas_call(k, out_shape=(jax.ShapeDtypeStruct((BLOCKS, LO, 16, EZ, W)...  63.2 us
    unnamed x14, local copies, waits for them, and re-layouts  8.37 us

profile of v2, /device:TPU:4, one launch (start us, length us, event | category | flops | bytes accessed | tf_op | source)
XLA Modules:
  0.0 72.2 jit_solution(13610552604147342745)
XLA Ops:
  0.6 0.0 copy-start
  0.6 1.6 %copy-done = bf16[8,16,16,512]{3,2,1,0:T(8,128)(2,1)S(1)} copy-done((bf16[8,16,16,512]{3,2,1,0:T(8,128)(2,1)S(1)}, bf16[8,16,16,512]{3,2,1,0:T(8,128)(2,1)}, u32[]{:S(2)}) %copy-start) | copy-done | bytes 2097176
  2.2 0.0 copy-start.1
  2.2 1.3 %copy-done.1 = bf16[729,729]{1,0:T(8,128)(2,1)S(1)} copy-done((bf16[729,729]{1,0:T(8,128)(2,1)S(1)}, bf16[729,729]{1,0:T(8,128)(2,1)}, u32[]{:S(2)}) %copy-start.1) | copy-done | bytes 1062906
  3.5 0.0 copy-start.2
  3.5 1.2 %copy-done.2 = bf16[2,8,16,16,128]{4,3,2,1,0:T(8,128)(2,1)S(1)} copy-done((bf16[2,8,16,16,128]{4,3,2,1,0:T(8,128)(2,1)S(1)}, bf16[2,8,16,16,128]{4,3,2,1,0:T(8,128)(2,1)}, u32[]{:S(2)}) %copy-start.2) | copy-done | bytes 1048600
  4.7 0.0 copy-start.3
  4.7 0.8 %copy-done.3 = f32[8,16,16]{2,1,0:T(8,128)S(1)} copy-done((f32[8,16,16]{2,1,0:T(8,128)S(1)}, f32[8,16,16]{2,1,0:T(8,128)}, u32[]{:S(2)}) %copy-start.3) | copy-done | bytes 8216
  5.5 0.0 copy-start.4
  5.5 0.8 %copy-done.4 = f32[8,16,16]{2,1,0:T(8,128)S(1)} copy-done((f32[8,16,16]{2,1,0:T(8,128)S(1)}, f32[8,16,16]{2,1,0:T(8,128)}, u32[]{:S(2)}) %copy-start.4) | copy-done | bytes 8216
  6.4 0.0 copy-start.5
  6.4 0.7 copy-done.5
  7.1 63.2 %shard_map.77 = (f32[2,8,16,16,128]{4,3,2,1,0:T(8,128)S(1)}, f32[16,256]{1,0:T(8,128)S(1)}) custom-call(bf16[2,8,16,16,128]{4,3,2,1,0:T(8,128)(2,1)S(1)} %copy-done.2, bf16[8,16,16,512]{3,2,1,0:T(8,128)(2,1)S(1)} %copy-done, f32[8,16,16]{2,1,0:T(8,128)S(1)} %copy-done.3, f32[8,16,16]{2,1,0:T(8,128)S(1)} %copy-done.4, bf16[729,729]{1,0:T(8,128)(2,1)S(1)} %copy-done.1, ...), custom_call_target="tpu_custom_call" | custom-call | tf_op jit(solution)/shard_map/pallas_call | solution.py:380
  70.3 1.3 %copy.10 = f32[2,8,16,16,128]{4,3,2,1,0:T(8,128)} copy(f32[2,8,16,16,128]{4,3,2,1,0:T(8,128)S(1)} %get-tuple-element.4) | data formatting | bytes 4194304
  71.6 0.6 copy.11
Async XLA Ops:
  0.6 1.6 %copy-start = (bf16[8,16,16,512]{3,2,1,0:T(8,128)(2,1)S(1)}, bf16[8,16,16,512]{3,2,1,0:T(8,128)(2,1)}, u32[]{:S(2)}) copy-start(bf16[8,16,16,512]{3,2,1,0:T(8,128)(2,1)} %refs_1_.1) | copy-start | bytes 6291460
  2.2 1.3 %copy-start.1 = (bf16[729,729]{1,0:T(8,128)(2,1)S(1)}, bf16[729,729]{1,0:T(8,128)(2,1)}, u32[]{:S(2)}) copy-start(bf16[729,729]{1,0:T(8,128)(2,1)} %refs_4_.1) | copy-start | bytes 3188650
  3.5 1.2 %copy-start.2 = (bf16[2,8,16,16,128]{4,3,2,1,0:T(8,128)(2,1)S(1)}, bf16[2,8,16,16,128]{4,3,2,1,0:T(8,128)(2,1)}, u32[]{:S(2)}) copy-start(bf16[2,8,16,16,128]{4,3,2,1,0:T(8,128)(2,1)} %refs_0_.1) | copy-start | bytes 3145732
  4.7 0.8 %copy-start.3 = (f32[8,16,16]{2,1,0:T(8,128)S(1)}, f32[8,16,16]{2,1,0:T(8,128)}, u32[]{:S(2)}) copy-start(f32[8,16,16]{2,1,0:T(8,128)} %refs_2_.1) | copy-start | bytes 24580
  5.5 0.8 %copy-start.4 = (f32[8,16,16]{2,1,0:T(8,128)S(1)}, f32[8,16,16]{2,1,0:T(8,128)}, u32[]{:S(2)}) copy-start(f32[8,16,16]{2,1,0:T(8,128)} %refs_3_.1) | copy-start | bytes 24580
  6.4 0.7 copy-start.5

commit v3 on v2

--- a/solution.py
+++ b/solution.py
@@ -22,7 +22,8 @@
 
 
 def kernel(
-    norm_scale, vec, res, mass, pot, amat, conn, out, margin,
+    norm_scale, vec_in, res, mass_in, pot_in, amat_in, conn_in, out, margin,
+    vec, mass, pot, amat, conn,
     ap, ac, acc, uf, y, im, bt, ub, wp, mloc, rs, posr, ct,
     xh, yh, dh, cx, cy_, cd, sx, sy, rx, ry, rd,
     m1s, m1r, m2s, m2r, m3s, m3r, m4s, m4r,
@@ -54,6 +55,14 @@
     greeted = neighbours + partner + row + column + group
     for device in greeted:
         pl.semaphore_signal(barrier, inc=1, device_id=device, device_id_type=MESH)
+    loads = [
+        pltpu.make_async_copy(src, dst, lsem.at[n + 1])
+        for n, (src, dst) in enumerate(
+            [(mass_in, mass), (pot_in, pot), (conn_in, conn), (amat_in, amat), (vec_in, vec)]
+        )
+    ]
+    for copy in loads:
+        copy.start()
     load = pltpu.make_async_copy(res, rs.at[pl.ds(0, LO), pl.ds(0, 16)], lsem.at[0])
     load.start()
 
@@ -62,6 +71,8 @@
             src_ref=src, dst_ref=dst, send_sem=ssem, recv_sem=rsem, device_id=device, device_id_type=MESH
         )
 
+    for copy in loads:
+        copy.wait()
     ct[0] = mass[...].reshape(LO * 16, EZ).T
     ct[1] = pot[...].reshape(LO * 16, EZ).T
 
@@ -112,11 +123,12 @@
     for copy in halo:
         copy.start()
     rhalo = [
-        remote(res.at[0], rs.at[LO, pl.ds(0, 16)], hs_sem.at[6], hr_sem.at[6], (pm, q)),
         remote(res.at[:, 0], rs.at[pl.ds(0, LO), 16], hs_sem.at[7], hr_sem.at[7], (p, qm)),
+        remote(res.at[0, pl.ds(0, 8)], rs.at[LO, pl.ds(0, 8)], hs_sem.at[6], hr_sem.at[6], (pm, q)),
         remote(res.at[0, 0], rs.at[LO, 16], hs_sem.at[8], hr_sem.at[8], (pm, qm)),
+        remote(res.at[0, pl.ds(8, 8)], rs.at[LO, pl.ds(8, 8)], hs_sem.at[9], hr_sem.at[9], (pm, q)),
     ]
-    for copy in rhalo:
+    for copy in rhalo[:2]:
         copy.start()
 
     def fill(i, carry):
@@ -127,7 +139,6 @@
         return carry
 
     lax.fori_loop(0, LO, fill, 0)
-    y[1] = jnp.zeros_like(y[1])
     lax.fori_loop(1, NCELL, permute, 0)
 
     for copy in halo:
@@ -148,39 +159,33 @@
         y[0, b, LO, 16] = value
         uf[b, LO, 16] = value * im[LO, 16]
 
-    low, high = pl.ds(0, 8), pl.ds(8, 9)
-
-    def exchange(d, part):
-        if part == 0:
-            plan = [
-                (0, sx.at[d, 0, :, low], rx.at[d, 1, :, low], (pm, q)),
-                (1, sx.at[d, 1, :, low], rx.at[d, 0, :, low], (pp, q)),
-                (2, sy.at[d, 0], ry.at[d, 1], (p, qm)),
-                (4, sx.at[d, 0, :, 0], rd.at[d, 3], (pm, qm)),
-                (7, sx.at[d, 1, :, 0], rd.at[d, 1], (pp, qm)),
-            ]
-            wanted = (1,)
-        else:
-            plan = [
-                (8, sx.at[d, 0, :, high], rx.at[d, 1, :, high], (pm, q)),
-                (9, sx.at[d, 1, :, high], rx.at[d, 0, :, high], (pp, q)),
-                (3, sy.at[d, 1], ry.at[d, 0], (p, qp)),
-                (5, sx.at[d, 1, :, 16], rd.at[d, 0], (pp, qp)),
-                (6, sx.at[d, 0, :, 16], rd.at[d, 2], (pm, qp)),
-            ]
-            wanted = (9, 3, 5)
-        last = isinstance(d, int) and d == DEGREE - 1
+    def exchange(d, b):
+        plan = [
+            (sx.at[d, 1, b, 16], rd.at[d, 0, b], (pp, qp)),
+            (sx.at[d, 0, b, 0], rd.at[d, 3, b], (pm, qm)),
+            (sx.at[d, 0, b, 16], rd.at[d, 2, b], (pm, qp)),
+            (sx.at[d, 1, b, 0], rd.at[d, 1, b], (pp, qm)),
+            (sy.at[d, 1, b], ry.at[d, 0, b], (p, qp)),
+            (sy.at[d, 0, b], ry.at[d, 1, b], (p, qm)),
+            (sx.at[d, 1, b], rx.at[d, 0, b], (pp, q)),
+            (sx.at[d, 0, b], rx.at[d, 1, b], (pm, q)),
+        ]
+        wanted = (0, 4, 6) if d == DEGREE - 1 else range(8)
         return [
-            remote(s, t, es_sem.at[d, n], er_sem.at[d, n], to) for n, s, t, to in plan if n in wanted or not last
+            remote(s, t, es_sem.at[d, b, n], er_sem.at[d, b, n], to)
+            for n, (s, t, to) in enumerate(plan)
+            if n in wanted
         ]
 
-    def cells(d, cy):
-        for cz in range(2):
-            c = cy * 2 + cz
-            kp = (8 * cz + 8) % 16
-            for b in range(BLOCKS):
-                flat = uf.at[b].reshape(EX * EY * EZ, W)
-                main = uf[b, :, 8 * cy : 8 * cy + 9, 8 * cz : 8 * cz + 8, :].reshape(648, W)
+    def cells(d, b):
+        flat = uf.at[b].reshape(EX * EY * EZ, W)
+        total = acc.at[b].reshape(EX * EY * EZ, W)
+        for cy in range(2):
+            for cz in range(2):
+                c = cy * 2 + cz
+                kp = (8 * cz + 8) % 16
+                ks = slice(8 * cz, 8 * cz + 8)
+                main = uf[b, :, 8 * cy : 8 * cy + 9, ks, :].reshape(648, W)
                 planes = [flat[pl.ds((i * EY + 8 * cy) * EZ + kp, 8, EZ), :] for i in range(EX)]
                 start = (8 * cy + 8) * EZ + kp
                 line = flat[pl.ds(start, 8, EY * EZ), :]
@@ -188,103 +193,92 @@
                 first = lax.broadcasted_iota(jnp.int32, (8, W), 0) == 0
                 last = jnp.where(first, jnp.broadcast_to(last, (8, W)), 0.0)
                 whole = jnp.concatenate([main] + planes + [line, last, jnp.zeros((32, W), F32)], axis=0)
-                ub[c, :, b * W : (b + 1) * W] = whole.astype(BF16)
-            w = jnp.dot(ac[c], ub[c], preferred_element_type=F32)
-            wp[c] = w[648:]
-            for b in range(BLOCKS):
-                block = w[:648, b * W : (b + 1) * W].reshape(EX, 9, 8, W)
-                ks = slice(8 * cz, 8 * cz + 8)
+                ub[b, c] = whole.astype(BF16)
+                w = jnp.dot(ac[c], ub[b, c], preferred_element_type=F32)
+                wp[b, c] = w[648:]
+                block = w[:648].reshape(EX, 9, 8, W)
                 if cy == 0:
                     acc[b, :, 0:9, ks, :] = block
                 else:
                     acc[b, :, 8, ks, :] += block[:, 0]
                     acc[b, :, 9:17, ks, :] = block[:, 1:]
-        for cz in range(2):
-            c = cy * 2 + cz
-            kp = (8 * cz + 8) % 16
-            for b in range(BLOCKS):
-                flat = acc.at[b].reshape(EX * EY * EZ, W)
-                cols = slice(b * W, (b + 1) * W)
+            for cz in range(2):
+                c = cy * 2 + cz
+                kp = (8 * cz + 8) % 16
                 for i in range(EX):
                     where = pl.ds((i * EY + 8 * cy) * EZ + kp, 8, EZ)
-                    flat[where, :] = flat[where, :] + wp[c, 8 * i : 8 * i + 8, cols]
+                    total[where, :] = total[where, :] + wp[b, c, 8 * i : 8 * i + 8]
                 start = (8 * cy + 8) * EZ + kp
                 where = pl.ds(start, 8, EY * EZ)
-                flat[where, :] = flat[where, :] + wp[c, 72:80, cols]
+                total[where, :] = total[where, :] + wp[b, c, 72:80]
                 where = pl.ds(start + 8 * EY * EZ, 1)
-                flat[where, :] = flat[where, :] + wp[c, 80:81, cols]
-        js = slice(0, 8) if cy == 0 else slice(8, 17)
-        for b in range(BLOCKS):
-            sx[d, 0, b, js] = acc[b, 0, js].astype(BF16)
-            sx[d, 1, b, js] = acc[b, LO, js].astype(BF16)
-            sy[d, cy, b] = acc[b, :, 16 * cy].astype(BF16)
-        copies = exchange(d, cy)
-        for copy in copies:
+                total[where, :] = total[where, :] + wp[b, c, 80:81]
+        sx[d, 0, b] = acc[b, 0].astype(BF16)
+        sx[d, 1, b] = acc[b, LO].astype(BF16)
+        sy[d, 0, b] = acc[b, :, 0].astype(BF16)
+        sy[d, 1, b] = acc[b, :, 16].astype(BF16)
+        for copy in exchange(d, b):
             copy.start()
-        return copies
-
-    def apply(d, now, later, scale, keep, close):
-        copies = cells(d, 0) + cells(d, 1)
+
+    def update(d, b):
+        now, later = d % 2, (d + 1) % 2
 
         def inner(i, carry):
-            for b in range(BLOCKS):
-                m = im[i]
-                fresh = scale * (acc[b, i] * (m * (1.0 / half_width)) + bt[i] * y[now, b, i]) - keep * y[later, b, i]
-                y[later, b, i] = fresh
+            m = im[i]
+            fresh = acc[b, i] * (m * (1.0 / half_width)) + bt[i] * y[now, b, i]
+            if d > 0:
+                fresh = 2.0 * fresh - y[later, b, i]
+            y[later, b, i] = fresh
+            if d < DEGREE - 1:
                 uf[b, i] = fresh * m
             return carry
 
         lax.fori_loop(0, EX, inner, 0)
 
-        def add(b, i, j, part):
-            y[later, b, i, j] = y[later, b, i, j] + (scale * (1.0 / half_width)) * im[i, j] * part.astype(F32)
-
-        def refresh(b, i, j):
+    def arrive(d, b):
+        later = (d + 1) % 2
+        factor = (1.0 if d == 0 else 2.0) / half_width
+
+        def add(i, j, part):
+            y[later, b, i, j] = y[later, b, i, j] + factor * im[i, j] * part.astype(F32)
+
+        def refresh(i, j):
             uf[b, i, j] = y[later, b, i, j] * im[i, j]
 
-        def arrive():
-            for copy in copies:
-                copy.wait()
-            for b in range(BLOCKS):
-                add(b, 0, slice(0, 17), rx[d, 0, b])
-                add(b, slice(0, EX), 0, ry[d, 0, b])
-                add(b, 0, 0, rd[d, 0, b])
-                add(b, LO, slice(0, 17), rx[d, 1, b])
-                add(b, slice(0, EX), 16, ry[d, 1, b])
-                add(b, 0, 16, rd[d, 1, b])
-                add(b, LO, 0, rd[d, 2, b])
-                add(b, LO, 16, rd[d, 3, b])
-                refresh(b, 0, slice(0, 17))
-                refresh(b, LO, slice(0, 17))
-                refresh(b, slice(1, LO), 0)
-                refresh(b, slice(1, LO), 16)
-
-        def arrive_last():
-            for copy in copies:
-                copy.wait()
-            for b in range(BLOCKS):
-                add(b, 0, slice(0, 16), rx[d, 0, b, 0:16])
-                add(b, slice(0, LO), 0, ry[d, 0, b, 0:LO])
-                add(b, 0, 0, rd[d, 0, b])
-
-        if close:
-            arrive()
-            return None
-        return arrive_last
-
-    def step(d, carry):
-        scale = jnp.where(d == 0, 1.0, 2.0).astype(F32)
-        keep = jnp.where(d == 0, 0.0, 1.0).astype(F32)
-        apply(d, lax.rem(d, 2), lax.rem(d + 1, 2), scale, keep, True)
-        return carry
-
-    lax.fori_loop(0, DEGREE - 1, step, 0)
+        for copy in exchange(d, b):
+            copy.wait()
+        if d == DEGREE - 1:
+            add(0, slice(0, 16), rx[d, 0, b, 0:16])
+            add(slice(0, LO), 0, ry[d, 0, b, 0:LO])
+            add(0, 0, rd[d, 0, b])
+            return
+        add(0, slice(0, 17), rx[d, 0, b])
+        add(slice(0, EX), 0, ry[d, 0, b])
+        add(0, 0, rd[d, 0, b])
+        add(LO, slice(0, 17), rx[d, 1, b])
+        add(slice(0, EX), 16, ry[d, 1, b])
+        add(0, 16, rd[d, 1, b])
+        add(LO, 0, rd[d, 2, b])
+        add(LO, 16, rd[d, 3, b])
+        refresh(0, slice(0, 17))
+        refresh(LO, slice(0, 17))
+        refresh(slice(1, LO), 0)
+        refresh(slice(1, LO), 16)
+
+    for d in range(DEGREE):
+        for b in range(BLOCKS):
+            if d > 0:
+                arrive(d - 1, b)
+            if d == DEGREE - 1:
+                for side in range(2):
+                    y[side, b, LO] = jnp.zeros((EY, EZ, W), F32)
+                    y[side, b, 0:LO, 16] = jnp.zeros((LO, EZ, W), F32)
+            cells(d, b)
+            if d == 0 and b == BLOCKS - 1:
+                for copy in rhalo[2:]:
+                    copy.start()
+            update(d, b)
     final = DEGREE % 2
-    y[1 - final, :, LO] = jnp.zeros((BLOCKS, EY, EZ, W), F32)
-    y[final, :, LO] = jnp.zeros((BLOCKS, EY, EZ, W), F32)
-    y[1 - final, :, 0:LO, 16] = jnp.zeros((BLOCKS, LO, EZ, W), F32)
-    y[final, :, 0:LO, 16] = jnp.zeros((BLOCKS, LO, EZ, W), F32)
-    arrive_last = apply(DEGREE - 1, 1 - final, final, 2.0, 1.0, False)
 
     load.wait()
     for copy in rhalo:
@@ -321,7 +315,8 @@
     copies = [remote(m2s.at[k], m2r.at[k], s2.at[k], r2.at[k], row[k]) for k in range(NXC - 1)]
     for copy in copies:
         copy.start()
-    arrive_last()
+    for b in range(BLOCKS):
+        arrive(DEGREE - 1, b)
     writes = [
         pltpu.make_async_copy(y.at[final, b, pl.ds(0, LO), pl.ds(0, 16)], out.at[b], osem.at[b])
         for b in range(BLOCKS)
@@ -370,7 +365,6 @@
     nz = ZL * ZH
     rows = 16 * ndy
     vmem = pl.BlockSpec(memory_space=pltpu.VMEM)
-    hbm = pl.BlockSpec(memory_space=pl.ANY)
     dma = pltpu.SemaphoreType.DMA
 
     def k(*refs):
@@ -383,9 +377,14 @@
             jax.ShapeDtypeStruct((BLOCKS, LO, 16, EZ, W), F32),
             jax.ShapeDtypeStruct((16, BLOCKS * W), F32),
         ),
-        in_specs=[vmem, hbm, vmem, vmem, vmem, vmem],
-        out_specs=(hbm, vmem),
+        in_specs=[pl.BlockSpec(memory_space=pltpu.HBM)] * 6,
+        out_specs=(pl.BlockSpec(memory_space=pl.ANY), vmem),
         scratch_shapes=[
+            pltpu.VMEM(vectors.shape, BF16),
+            pltpu.VMEM(inv_mass.shape, F32),
+            pltpu.VMEM(potential.shape, F32),
+            pltpu.VMEM(cell_matrix.shape, BF16),
+            pltpu.VMEM(connectivity.shape, jnp.int32),
             pltpu.VMEM((KP, KP), BF16),
             pltpu.VMEM((NCELL, KP, KP), BF16),
             pltpu.VMEM(state, F32),
@@ -393,8 +392,8 @@
             pltpu.VMEM((2, *state), F32),
             pltpu.VMEM((EX, EY, EZ, W), F32),
             pltpu.VMEM((EX, EY, EZ, W), F32),
-            pltpu.VMEM((NCELL, KP, BLOCKS * W), BF16),
-            pltpu.VMEM((NCELL, KP - 648, BLOCKS * W), F32),
+            pltpu.VMEM((BLOCKS, NCELL, KP, W), BF16),
+            pltpu.VMEM((BLOCKS, NCELL, KP - 648, W), F32),
             pltpu.VMEM((rows, BLOCKS * W), F32),
             pltpu.VMEM((EX, EY, EZ, nres), BF16),
             pltpu.VMEM((NCELL, 1, KP), jnp.int32),
@@ -418,12 +417,12 @@
             pltpu.VMEM((nz - 1, 8, BLOCKS * W), F32),
             pltpu.VMEM((8, BLOCKS * W), F32),
             pltpu.VMEM((ndx, 8, BLOCKS * W), F32),
-            dma((9,)), dma((9,)), dma((DEGREE, 10)), dma((DEGREE, 10)),
+            dma((10,)), dma((10,)), dma((DEGREE, BLOCKS, 8)), dma((DEGREE, BLOCKS, 8)),
             dma((1,)), dma((1,)), dma((NXC - 1,)), dma((NXC - 1,)),
-            dma((nz - 1,)), dma((nz - 1,)), dma((ndx - 1,)), dma((ndx - 1,)), dma((BLOCKS,)), dma((1,)),
+            dma((nz - 1,)), dma((nz - 1,)), dma((ndx - 1,)), dma((ndx - 1,)), dma((BLOCKS,)), dma((6,)),
         ],
         compiler_params=pltpu.CompilerParams(
-            collective_id=0, has_side_effects=True, vmem_limit_bytes=44 * 1024 * 1024
+            collective_id=0, has_side_effects=True, vmem_limit_bytes=62914560
         ),
     )(vectors, resident, inv_mass, potential, cell_matrix, connectivity)
 

time: 72.5 us -> 61.9 us (0.85)
  Pallas kernels: 63.2 us -> 57.4 us
  local copies, waits for them, and re-layouts: 8.37 us -> 3.71 us
    pallas_call x1, Pallas kernels: 63.2 us -> 57.4 us  [body(): pl.pallas_call(k, out_shape=(jax.ShapeDtypeStruct((BLOCKS, LO, 16, EZ, W)...]
    unnamed x14 -> x4, local copies, waits for them, and re-layouts: 8.37 us -> 3.71 us
where the time goes in v3:
time: 61.9 us; the launch traced here: 61.8 us
  Pallas kernels  57.4 us (93%)
  local copies, waits for them, and re-layouts  3.71 us (6%)
  between operations  0.65 us (1%)
    pallas_call x1, Pallas kernels, body(): pl.pallas_call(k, out_shape=(jax.ShapeDtypeStruct((BLOCKS, LO, 16, EZ, W)...  57.4 us
    unnamed x4, local copies, waits for them, and re-layouts  3.71 us

profile of v3, /device:TPU:4, one launch (start us, length us, event | category | flops | bytes accessed | tf_op | source)
XLA Modules:
  0.0 61.8 jit_solution(13165405371454178416)
XLA Ops:
  0.6 57.4 %shard_map.77 = (f32[2,8,16,16,128]{4,3,2,1,0:T(8,128)}, f32[16,256]{1,0:T(8,128)}) custom-call(bf16[2,8,16,16,128]{4,3,2,1,0:T(8,128)(2,1)} %refs_0_.1, bf16[8,16,16,512]{3,2,1,0:T(8,128)(2,1)} %refs_1_.1, f32[8,16,16]{2,1,0:T(8,128)} %refs_2_.1, f32[8,16,16]{2,1,0:T(8,128)} %refs_3_.1, bf16[729,729]{1,0:T(8,128)(2,1)} %refs_4_.1, s32[1,1,4,729]{3,2,1,0:T(4,128)} %refs_5_.1), custom_call_target="tpu_custom_call" | custom-call | tf_op jit(solution)/shard_map/pallas_call | solution.py:374
  58.1 0.0 copy-start
  58.1 3.1 %copy.10 = f32[2,8,16,16,128]{4,3,2,1,0:T(8,128)} copy(f32[2,8,16,16,128]{4,3,2,1,0:T(8,128)} %get-tuple-element.4) | data formatting | bytes 4194304
  61.2 0.0 copy-done
  61.2 0.6 copy.11
Async XLA Ops:
  58.1 3.1 %copy-start = (f32[16,256]{1,0:T(8,128)S(1)}, f32[16,256]{1,0:T(8,128)}, u32[]{:S(2)}) copy-start(f32[16,256]{1,0:T(8,128)} %get-tuple-element.5) | copy-start | bytes 49156

commit v4 on v3

--- a/solution.py
+++ b/solution.py
@@ -24,7 +24,7 @@
 def kernel(
     norm_scale, vec_in, res, mass_in, pot_in, amat_in, conn_in, out, margin,
     vec, mass, pot, amat, conn,
-    ap, ac, acc, uf, y, im, bt, ub, wp, mloc, rs, posr, ct,
+    ap, ac, acc, uf, y, im, bt, ub, wp, mloc, rs, rt, vb, posr, ct,
     xh, yh, dh, cx, cy_, cd, sx, sy, rx, ry, rd,
     m1s, m1r, m2s, m2r, m3s, m3r, m4s, m4r,
     hs_sem, hr_sem, es_sem, er_sem, s1, r1, s2, r2, s3, r3, s4, r4, osem, lsem,
@@ -139,6 +139,10 @@
         return carry
 
     lax.fori_loop(0, LO, fill, 0)
+    tail = EX * 256
+    rt[:, tail:] = jnp.zeros((rt.shape[0], 256), BF16)
+    for b in range(BLOCKS):
+        vb[b, tail:] = jnp.zeros((256, W), BF16)
     lax.fori_loop(1, NCELL, permute, 0)
 
     for copy in halo:
@@ -231,6 +235,9 @@
             y[later, b, i] = fresh
             if d < DEGREE - 1:
                 uf[b, i] = fresh * m
+            else:
+                vb[b, pl.ds(pl.multiple_of(i * 256, 256), 256)] = fresh[0:16].reshape(256, W).astype(BF16)
+                vb[b, pl.ds(pl.multiple_of(tail + i * EZ, EZ), EZ)] = fresh[16].astype(BF16)
             return carry
 
         lax.fori_loop(0, EX, inner, 0)
@@ -265,6 +272,45 @@
         refresh(slice(1, LO), 0)
         refresh(slice(1, LO), 16)
 
+    nres = rs.shape[-1]
+    span = CORES * 16
+
+    def turn_own():
+        load.wait()
+        for i in range(LO):
+            rt[:, i * 256 : (i + 1) * 256] = rs[i, 0:16].reshape(256, nres).T
+
+    def turn_halo():
+        for copy in rhalo:
+            copy.wait()
+        rt[:, LO * 256 : EX * 256] = rs[LO, 0:16].reshape(256, nres).T
+        rt[:, tail : tail + EX * EZ] = rs[:, 16].reshape(EX * EZ, nres).T
+
+    def both(b, g):
+        own = mloc[b, pl.ds(pl.multiple_of(g * span + core * 16, 16), 16), :]
+        return own + m1r[b, g].astype(F32)
+
+    def to_partner(b):
+        return remote(m1s.at[b], m1r.at[b], s1.at[b], r1.at[b], partner[0])
+
+    def to_row(b):
+        return [remote(m2s.at[b, k], m2r.at[b, k], s2.at[b, k], r2.at[b, k], row[k]) for k in range(NXC - 1)]
+
+    def first(b):
+        mloc[b] = jnp.dot(rt[...], vb[b], preferred_element_type=F32) * norm_scale
+        for g in range(ZH * NXC):
+            where = pl.ds(pl.multiple_of(g * span + (CORES - 1 - core) * 16, 16), 16)
+            m1s[b, g] = mloc[b, where, :].astype(BF16)
+        to_partner(b).start()
+
+    def second(b):
+        to_partner(b).wait()
+        for zv in range(ZH):
+            for k in range(1, NXC):
+                m2s[b, k - 1, zv] = both(b, zv * NXC + (xc + k) % NXC).astype(BF16)
+        for copy in to_row(b):
+            copy.start()
+
     for d in range(DEGREE):
         for b in range(BLOCKS):
             if d > 0:
@@ -277,44 +323,17 @@
             if d == 0 and b == BLOCKS - 1:
                 for copy in rhalo[2:]:
                     copy.start()
+            if d == DEGREE - 1 and b > 0:
+                second(b - 1)
             update(d, b)
+            if d == DEGREE - 1:
+                first(b)
+        if d == 0:
+            turn_own()
+        if d == 1:
+            turn_halo()
+    second(BLOCKS - 1)
     final = DEGREE % 2
-
-    load.wait()
-    for copy in rhalo:
-        copy.wait()
-    nres = rs.shape[-1]
-    right = jnp.concatenate([y[final, b, :, 16].reshape(EX * EZ, W).astype(BF16) for b in range(BLOCKS)], axis=1)
-    mloc[...] = lax.dot_general(
-        rs[:, 16].reshape(EX * EZ, nres), right, (((0,), (0,)), ((), ())), preferred_element_type=F32
-    )
-
-    def product(i, carry):
-        cols = [y[final, b, i, 0:16].reshape(256, W).astype(BF16) for b in range(BLOCKS)]
-        right = jnp.concatenate(cols, axis=1)
-        left = rs[i, 0:16].reshape(256, nres)
-        mloc[...] += lax.dot_general(left, right, (((0,), (0,)), ((), ())), preferred_element_type=F32)
-        return carry
-
-    lax.fori_loop(0, EX, product, 0)
-
-    span = CORES * 16
-    for g in range(ZH * NXC):
-        m1s[g] = (mloc[pl.ds(pl.multiple_of(g * span + (CORES - 1 - core) * 16, 16), 16), :] * norm_scale).astype(BF16)
-    copy = remote(m1s, m1r, s1.at[0], r1.at[0], partner[0])
-    copy.start()
-    copy.wait()
-
-    def both(g):
-        own = mloc[pl.ds(pl.multiple_of(g * span + core * 16, 16), 16), :] * norm_scale
-        return own + m1r[g].astype(F32)
-
-    for zv in range(ZH):
-        for k in range(1, NXC):
-            m2s[k - 1, zv] = both(zv * NXC + (xc + k) % NXC).astype(BF16)
-    copies = [remote(m2s.at[k], m2r.at[k], s2.at[k], r2.at[k], row[k]) for k in range(NXC - 1)]
-    for copy in copies:
-        copy.start()
     for b in range(BLOCKS):
         arrive(DEGREE - 1, b)
     writes = [
@@ -323,14 +342,15 @@
     ]
     for copy in writes:
         copy.start()
-    for copy in copies:
-        copy.wait()
-    for zv in range(ZH):
-        total = both(zv * NXC + xc)
-        for k in range(NXC - 1):
-            total = total + m2r[k, zv].astype(F32)
-        for half in range(ZL):
-            m3s[zv * ZL + half] = total[half * 8 : half * 8 + 8]
+    for b in range(BLOCKS):
+        for copy in to_row(b):
+            copy.wait()
+        for zv in range(ZH):
+            total = both(b, zv * NXC + xc)
+            for k in range(NXC - 1):
+                total = total + m2r[b, k, zv].astype(F32)
+            for half in range(ZL):
+                m3s[zv * ZL + half, :, b * W : (b + 1) * W] = total[half * 8 : half * 8 + 8]
     copies = [
         remote(m3s.at[(zi + k + 1) % nz], m3r.at[k], s3.at[k], r3.at[k], column[k]) for k in range(nz - 1)
     ]
@@ -371,7 +391,7 @@
         kernel(norm_scale, *refs)
 
     state = (BLOCKS, EX, EY, EZ, W)
-    return pl.pallas_call(
+    results = pl.pallas_call(
         k,
         out_shape=(
             jax.ShapeDtypeStruct((BLOCKS, LO, 16, EZ, W), F32),
@@ -394,8 +414,10 @@
             pltpu.VMEM((EX, EY, EZ, W), F32),
             pltpu.VMEM((BLOCKS, NCELL, KP, W), BF16),
             pltpu.VMEM((BLOCKS, NCELL, KP - 648, W), F32),
-            pltpu.VMEM((rows, BLOCKS * W), F32),
+            pltpu.VMEM((BLOCKS, rows, W), F32),
             pltpu.VMEM((EX, EY, EZ, nres), BF16),
+            pltpu.VMEM((nres, (EX + 1) * 256), BF16),
+            pltpu.VMEM((BLOCKS, (EX + 1) * 256, W), BF16),
             pltpu.VMEM((NCELL, 1, KP), jnp.int32),
             pltpu.VMEM((2, EZ, LO * 16), F32),
             pltpu.VMEM((BLOCKS, 16, EZ, W), BF16),
@@ -409,22 +431,52 @@
             pltpu.VMEM((DEGREE, 2, BLOCKS, EY, EZ, W), BF16),
             pltpu.VMEM((DEGREE, 2, BLOCKS, EX, EZ, W), BF16),
             pltpu.VMEM((DEGREE, 4, BLOCKS, EZ, W), BF16),
-            pltpu.VMEM((ZH * NXC, 16, BLOCKS * W), BF16),
-            pltpu.VMEM((ZH * NXC, 16, BLOCKS * W), BF16),
-            pltpu.VMEM((NXC - 1, ZH, 16, BLOCKS * W), BF16),
-            pltpu.VMEM((NXC - 1, ZH, 16, BLOCKS * W), BF16),
+            pltpu.VMEM((BLOCKS, ZH * NXC, 16, W), BF16),
+            pltpu.VMEM((BLOCKS, ZH * NXC, 16, W), BF16),
+            pltpu.VMEM((BLOCKS, NXC - 1, ZH, 16, W), BF16),
+            pltpu.VMEM((BLOCKS, NXC - 1, ZH, 16, W), BF16),
             pltpu.VMEM((nz, 8, BLOCKS * W), F32),
             pltpu.VMEM((nz - 1, 8, BLOCKS * W), F32),
             pltpu.VMEM((8, BLOCKS * W), F32),
             pltpu.VMEM((ndx, 8, BLOCKS * W), F32),
             dma((10,)), dma((10,)), dma((DEGREE, BLOCKS, 8)), dma((DEGREE, BLOCKS, 8)),
-            dma((1,)), dma((1,)), dma((NXC - 1,)), dma((NXC - 1,)),
+            dma((BLOCKS,)), dma((BLOCKS,)), dma((BLOCKS, NXC - 1)), dma((BLOCKS, NXC - 1)),
             dma((nz - 1,)), dma((nz - 1,)), dma((ndx - 1,)), dma((ndx - 1,)), dma((BLOCKS,)), dma((6,)),
         ],
         compiler_params=pltpu.CompilerParams(
             collective_id=0, has_side_effects=True, vmem_limit_bytes=62914560
         ),
     )(vectors, resident, inv_mass, potential, cell_matrix, connectivity)
+    in_hbm = pl.BlockSpec(memory_space=pltpu.HBM)
+    return pl.pallas_call(
+        hand_on,
+        out_shape=tuple(jax.ShapeDtypeStruct(r.shape, F32) for r in results),
+        in_specs=[in_hbm] * 2,
+        out_specs=(in_hbm, in_hbm),
+        scratch_shapes=[pltpu.VMEM(r.shape, F32) for r in results] + [dma((PIECES + 1,)), dma((PIECES + 1,))],
+        compiler_params=pltpu.CompilerParams(vmem_limit_bytes=60 * 1024 * 1024),
+    )(*results)
+
+
+PIECES = 8
+
+
+def hand_on(values, rows, values_out, rows_out, held, held_rows, isem, osem):
+    plan = [(rows, held_rows, rows_out)]
+    step = BLOCKS * LO // PIECES
+    for n in range(PIECES):
+        at = (n * step // LO, pl.ds(n * step % LO, step))
+        plan.append((values.at[at], held.at[at], values_out.at[at]))
+    copies = []
+    for n, (src, mid, dst) in enumerate(plan):
+        copies.append((pltpu.make_async_copy(src, mid, isem.at[n]), pltpu.make_async_copy(mid, dst, osem.at[n])))
+    for into, _ in copies:
+        into.start()
+    for into, back in copies:
+        into.wait()
+        back.start()
+    for _, back in copies:
+        back.wait()
 
 
 def solution(mesh):

time: 61.9 us -> 61.2 us (0.989); the launches traced: 61.8 us -> 60.5 us
  local copies, waits for them, and re-layouts: 3.71 us -> 0 us
  Pallas kernels: 57.4 us -> 59.7 us
    unnamed x4 -> x0, local copies, waits for them, and re-layouts: 3.71 us -> none
    pallas_call x0 -> x1, Pallas kernels: none -> 2.43 us  [body(): pl.pallas_call(hand_on, out_shape=tuple((jax.ShapeDtypeStruct(r.shape, F3...]
where the time goes in v4:
time: 61.2 us; the launch traced here: 60.5 us
  Pallas kernels  59.7 us (98%)
  between operations  0.8 us (1%)
    pallas_call x1, Pallas kernels, body(): pl.pallas_call(k, out_shape=(jax.ShapeDtypeStruct((BLOCKS, LO, 16, EZ, W)...  57.2 us
    pallas_call x1, Pallas kernels, body(): pl.pallas_call(hand_on, out_shape=tuple((jax.ShapeDtypeStruct(r.shape, F3...  2.43 us

profile of v4, /device:TPU:4, one launch (start us, length us, event | category | flops | bytes accessed | tf_op | source)
XLA Modules:
  0.0 60.5 jit_solution(6360993972493061594)
XLA Ops:
  0.6 57.2 %shard_map.77 = (f32[2,8,16,16,128]{4,3,2,1,0:T(8,128)}, f32[16,256]{1,0:T(8,128)}) custom-call(bf16[2,8,16,16,128]{4,3,2,1,0:T(8,128)(2,1)} %refs_0_.1, bf16[8,16,16,512]{3,2,1,0:T(8,128)(2,1)} %refs_1_.1, f32[8,16,16]{2,1,0:T(8,128)} %refs_2_.1, f32[8,16,16]{2,1,0:T(8,128)} %refs_3_.1, bf16[729,729]{1,0:T(8,128)(2,1)} %refs_4_.1, s32[1,1,4,729]{3,2,1,0:T(4,128)} %refs_5_.1), custom_call_target="tpu_custom_call" | custom-call | tf_op jit(solution)/shard_map/pallas_call | solution.py:394
  57.9 2.4 %shard_map.78 = (f32[2,8,16,16,128]{4,3,2,1,0:T(8,128)}, f32[16,256]{1,0:T(8,128)}) custom-call(f32[2,8,16,16,128]{4,3,2,1,0:T(8,128)} %get-tuple-element.4.values, f32[16,256]{1,0:T(8,128)} %get-tuple-element.5.rows), custom_call_target="tpu_custom_call" | custom-call | tf_op jit(solution)/shard_map/pallas_call | solution.py:451

commit v5 on v4

--- a/solution.py
+++ b/solution.py
@@ -26,7 +26,7 @@
     vec, mass, pot, amat, conn,
     ap, ac, acc, uf, y, im, bt, ub, wp, mloc, rs, rt, vb, posr, ct,
     xh, yh, dh, cx, cy_, cd, sx, sy, rx, ry, rd,
-    m1s, m1r, m2s, m2r, m3s, m3r, m4s, m4r,
+    m1s, m1r, m2s, m2r, m3f, m3s, m3r, m4s, m4r,
     hs_sem, hr_sem, es_sem, er_sem, s1, r1, s2, r2, s3, r3, s4, r4, osem, lsem,
 ):
     p = lax.axis_index("dx")
@@ -71,7 +71,7 @@
             src_ref=src, dst_ref=dst, send_sem=ssem, recv_sem=rsem, device_id=device, device_id_type=MESH
         )
 
-    for copy in loads:
+    for copy in loads[:3]:
         copy.wait()
     ct[0] = mass[...].reshape(LO * 16, EZ).T
     ct[1] = pot[...].reshape(LO * 16, EZ).T
@@ -90,7 +90,6 @@
     for c in range(NCELL):
         posr[c, :, 0:nc] = where[c : c + 1]
     ap[...] = jnp.zeros_like(ap)
-    ap[0:nc, 0:nc] = amat[...]
 
     def spread(tile, lane):
         return jnp.broadcast_to(tile[:, lane : lane + 1], (EZ, W))
@@ -103,10 +102,21 @@
         for j in range(16):
             coefs(i, j, spread(ct[0], i * 16 + j), spread(ct[1], i * 16 + j))
 
+    for copy in loads[3:]:
+        copy.wait()
+    ap[0:nc, 0:nc] = amat[...]
+
     def permute(c, carry):
         onehot = (lax.broadcasted_iota(jnp.int32, (KP, KP), 0) == posr[c]).astype(F32).astype(BF16)
         rows = jnp.dot(onehot, ap[...], preferred_element_type=F32).astype(BF16)
-        ac[c] = lax.dot_general(rows, onehot, (((1,), (1,)), ((), ())), preferred_element_type=F32).astype(BF16)
+        for col in range(KP // 256):
+            at = slice(col * 256, (col + 1) * 256)
+            upper = lax.dot_general(
+                rows[: (col + 1) * 256], onehot[at], (((1,), (1,)), ((), ())), preferred_element_type=F32
+            ).astype(BF16)
+            ac[c, 0 : (col + 1) * 256, at] = upper
+            for line in range(col):
+                ac[c, at, line * 256 : (line + 1) * 256] = upper[line * 256 : (line + 1) * 256].T
         return carry
 
     lax.fori_loop(0, 1, permute, 0)
@@ -350,7 +360,8 @@
             for k in range(NXC - 1):
                 total = total + m2r[b, k, zv].astype(F32)
             for half in range(ZL):
-                m3s[zv * ZL + half, :, b * W : (b + 1) * W] = total[half * 8 : half * 8 + 8]
+                m3f[zv * ZL + half, :, b * W : (b + 1) * W] = total[half * 8 : half * 8 + 8]
+                m3s[zv * ZL + half, :, b * W : (b + 1) * W] = total[half * 8 : half * 8 + 8].astype(BF16)
     copies = [
         remote(m3s.at[(zi + k + 1) % nz], m3r.at[k], s3.at[k], r3.at[k], column[k]) for k in range(nz - 1)
     ]
@@ -358,9 +369,9 @@
         copy.start()
     for copy in copies:
         copy.wait()
-    total = m3s[zi]
+    total = m3f[zi]
     for k in range(nz - 1):
-        total = total + m3r[k]
+        total = total + m3r[k].astype(F32)
     m4s[...] = total
     m4r[p] = total
     copies = [remote(m4s, m4r.at[p], s4.at[k], r4.at[k], group[k]) for k in range(ndx - 1)]
@@ -436,7 +447,8 @@
             pltpu.VMEM((BLOCKS, NXC - 1, ZH, 16, W), BF16),
             pltpu.VMEM((BLOCKS, NXC - 1, ZH, 16, W), BF16),
             pltpu.VMEM((nz, 8, BLOCKS * W), F32),
-            pltpu.VMEM((nz - 1, 8, BLOCKS * W), F32),
+            pltpu.VMEM((nz, 8, BLOCKS * W), BF16),
+            pltpu.VMEM((nz - 1, 8, BLOCKS * W), BF16),
             pltpu.VMEM((8, BLOCKS * W), F32),
             pltpu.VMEM((ndx, 8, BLOCKS * W), F32),
             dma((10,)), dma((10,)), dma((DEGREE, BLOCKS, 8)), dma((DEGREE, BLOCKS, 8)),

time: 61.2 us -> 61.3 us (level)
  no operation moved by 1% of the time
where the time goes in v5:
time: 61.3 us; the launch traced here: 60.5 us
  Pallas kernels  59.7 us (97%)
  between operations  0.8 us (1%)
    pallas_call x1, Pallas kernels, body(): pl.pallas_call(k, out_shape=(jax.ShapeDtypeStruct((BLOCKS, LO, 16, EZ, W)...  57.3 us
    pallas_call x1, Pallas kernels, body(): pl.pallas_call(hand_on, out_shape=tuple((jax.ShapeDtypeStruct(r.shape, F3...  2.43 us

profile of v5, /device:TPU:4, one launch (start us, length us, event | category | flops | bytes accessed | tf_op | source)
XLA Modules:
  0.0 60.5 jit_solution(18130684932077019954)
XLA Ops:
  0.6 57.3 %shard_map.77 = (f32[2,8,16,16,128]{4,3,2,1,0:T(8,128)}, f32[16,256]{1,0:T(8,128)}) custom-call(bf16[2,8,16,16,128]{4,3,2,1,0:T(8,128)(2,1)} %refs_0_.1, bf16[8,16,16,512]{3,2,1,0:T(8,128)(2,1)} %refs_1_.1, f32[8,16,16]{2,1,0:T(8,128)} %refs_2_.1, f32[8,16,16]{2,1,0:T(8,128)} %refs_3_.1, bf16[729,729]{1,0:T(8,128)(2,1)} %refs_4_.1, s32[1,1,4,729]{3,2,1,0:T(4,128)} %refs_5_.1), custom_call_target="tpu_custom_call" | custom-call | tf_op jit(solution)/shard_map/pallas_call | solution.py:405
  58.0 2.4 %shard_map.78 = (f32[2,8,16,16,128]{4,3,2,1,0:T(8,128)}, f32[16,256]{1,0:T(8,128)}) custom-call(f32[2,8,16,16,128]{4,3,2,1,0:T(8,128)} %get-tuple-element.4.values, f32[16,256]{1,0:T(8,128)} %get-tuple-element.5.rows), custom_call_target="tpu_custom_call" | custom-call | tf_op jit(solution)/shard_map/pallas_call | solution.py:463

commit v6 on v5

--- a/solution.py
+++ b/solution.py
@@ -24,9 +24,9 @@
 def kernel(
     norm_scale, vec_in, res, mass_in, pot_in, amat_in, conn_in, out, margin,
     vec, mass, pot, amat, conn,
-    ap, ac, acc, uf, y, im, bt, ub, wp, mloc, rs, rt, vb, posr, ct,
+    ap, ac, cl, sd, acc, uf, y, im, bt, ub, wp, mloc, rs, rt, vb, posr, ct,
     xh, yh, dh, cx, cy_, cd, sx, sy, rx, ry, rd,
-    m1s, m1r, m2s, m2r, m3f, m3s, m3r, m4s, m4r,
+    m1s, m1r, m2s, m2r, m3s, m3r, m4s, m4r,
     hs_sem, hr_sem, es_sem, er_sem, s1, r1, s2, r2, s3, r3, s4, r4, osem, lsem,
 ):
     p = lax.axis_index("dx")
@@ -154,6 +154,11 @@
     for b in range(BLOCKS):
         vb[b, tail:] = jnp.zeros((256, W), BF16)
     lax.fori_loop(1, NCELL, permute, 0)
+    for c in range(NCELL):
+        jo = 8 * (c // 2)
+        tops = [jo * 8, (72 + jo) * 8] + ([648, 648 + 64] if jo == 0 else [720, 728])
+        for n, top in enumerate(tops):
+            cl[c, 8 * n : 8 * n + 8] = ac[c, top : top + 8]
 
     for copy in halo:
         copy.wait()
@@ -175,10 +180,10 @@
 
     def exchange(d, b):
         plan = [
-            (sx.at[d, 1, b, 16], rd.at[d, 0, b], (pp, qp)),
-            (sx.at[d, 0, b, 0], rd.at[d, 3, b], (pm, qm)),
-            (sx.at[d, 0, b, 16], rd.at[d, 2, b], (pm, qp)),
-            (sx.at[d, 1, b, 0], rd.at[d, 1, b], (pp, qm)),
+            (sd.at[d, 3, b], rd.at[d, 0, b], (pp, qp)),
+            (sd.at[d, 0, b], rd.at[d, 3, b], (pm, qm)),
+            (sd.at[d, 1, b], rd.at[d, 2, b], (pm, qp)),
+            (sd.at[d, 2, b], rd.at[d, 1, b], (pp, qm)),
             (sy.at[d, 1, b], ry.at[d, 0, b], (p, qp)),
             (sy.at[d, 0, b], ry.at[d, 1, b], (p, qm)),
             (sx.at[d, 1, b], rx.at[d, 0, b], (pp, q)),
@@ -208,6 +213,22 @@
                 last = jnp.where(first, jnp.broadcast_to(last, (8, W)), 0.0)
                 whole = jnp.concatenate([main] + planes + [line, last, jnp.zeros((32, W), F32)], axis=0)
                 ub[b, c] = whole.astype(BF16)
+            ends = [jnp.dot(cl[cy * 2 + cz], ub[b, cy * 2 + cz], preferred_element_type=F32) for cz in range(2)]
+            place = lax.broadcasted_iota(jnp.int32, (EZ, W), 0)
+            for side in range(2):
+                edge = jnp.concatenate([e[8 * side : 8 * side + 8] for e in ends], axis=0)
+                at8 = jnp.broadcast_to(ends[0][16 + 8 * side : 17 + 8 * side], (EZ, W))
+                at0 = jnp.broadcast_to(ends[1][16 + 8 * side : 17 + 8 * side], (EZ, W))
+                edge = edge + jnp.where(place == 8, at8, 0.0) + jnp.where(place == 0, at0, 0.0)
+                sd[d, 2 * side + cy, b] = edge.astype(BF16)
+        copies = exchange(d, b)
+        far = 1 if d == DEGREE - 1 else 4
+        for copy in copies[:far]:
+            copy.start()
+        for cy in range(2):
+            for cz in range(2):
+                c = cy * 2 + cz
+                ks = slice(8 * cz, 8 * cz + 8)
                 w = jnp.dot(ac[c], ub[b, c], preferred_element_type=F32)
                 wp[b, c] = w[648:]
                 block = w[:648].reshape(EX, 9, 8, W)
@@ -231,7 +252,7 @@
         sx[d, 1, b] = acc[b, LO].astype(BF16)
         sy[d, 0, b] = acc[b, :, 0].astype(BF16)
         sy[d, 1, b] = acc[b, :, 16].astype(BF16)
-        for copy in exchange(d, b):
+        for copy in copies[far:]:
             copy.start()
 
     def update(d, b):
@@ -360,8 +381,7 @@
             for k in range(NXC - 1):
                 total = total + m2r[b, k, zv].astype(F32)
             for half in range(ZL):
-                m3f[zv * ZL + half, :, b * W : (b + 1) * W] = total[half * 8 : half * 8 + 8]
-                m3s[zv * ZL + half, :, b * W : (b + 1) * W] = total[half * 8 : half * 8 + 8].astype(BF16)
+                m3s[zv * ZL + half, :, b * W : (b + 1) * W] = total[half * 8 : half * 8 + 8]
     copies = [
         remote(m3s.at[(zi + k + 1) % nz], m3r.at[k], s3.at[k], r3.at[k], column[k]) for k in range(nz - 1)
     ]
@@ -369,9 +389,9 @@
         copy.start()
     for copy in copies:
         copy.wait()
-    total = m3f[zi]
+    total = m3s[zi]
     for k in range(nz - 1):
-        total = total + m3r[k].astype(F32)
+        total = total + m3r[k]
     m4s[...] = total
     m4r[p] = total
     copies = [remote(m4s, m4r.at[p], s4.at[k], r4.at[k], group[k]) for k in range(ndx - 1)]
@@ -418,6 +438,8 @@
             pltpu.VMEM(connectivity.shape, jnp.int32),
             pltpu.VMEM((KP, KP), BF16),
             pltpu.VMEM((NCELL, KP, KP), BF16),
+            pltpu.VMEM((NCELL, 32, KP), BF16),
+            pltpu.VMEM((DEGREE, 4, BLOCKS, EZ, W), BF16),
             pltpu.VMEM(state, F32),
             pltpu.VMEM(state, F32),
             pltpu.VMEM((2, *state), F32),
@@ -447,8 +469,7 @@
             pltpu.VMEM((BLOCKS, NXC - 1, ZH, 16, W), BF16),
             pltpu.VMEM((BLOCKS, NXC - 1, ZH, 16, W), BF16),
             pltpu.VMEM((nz, 8, BLOCKS * W), F32),
-            pltpu.VMEM((nz, 8, BLOCKS * W), BF16),
-            pltpu.VMEM((nz - 1, 8, BLOCKS * W), BF16),
+            pltpu.VMEM((nz - 1, 8, BLOCKS * W), F32),
             pltpu.VMEM((8, BLOCKS * W), F32),
             pltpu.VMEM((ndx, 8, BLOCKS * W), F32),
             dma((10,)), dma((10,)), dma((DEGREE, BLOCKS, 8)), dma((DEGREE, BLOCKS, 8)),

time: 61.3 us -> 62.2 us (1.015)
  Pallas kernels: 59.7 us -> 60.4 us
    pallas_call x1, Pallas kernels: 57.3 us -> 58 us  [body(): pl.pallas_call(k, out_shape=(jax.ShapeDtypeStruct((BLOCKS, LO, 16, EZ, W)...]
where the time goes in v6:
time: 62.2 us; the launch traced here: 61.2 us
  Pallas kernels  60.4 us (97%)
  between operations  0.8 us (1%)
    pallas_call x1, Pallas kernels, body(): pl.pallas_call(k, out_shape=(jax.ShapeDtypeStruct((BLOCKS, LO, 16, EZ, W)...  58 us
    pallas_call x1, Pallas kernels, body(): pl.pallas_call(hand_on, out_shape=tuple((jax.ShapeDtypeStruct(r.shape, F3...  2.43 us

profile of v6, /device:TPU:4, one launch (start us, length us, event | category | flops | bytes accessed | tf_op | source)
XLA Modules:
  0.0 61.2 jit_solution(4047630373381087396)
XLA Ops:
  0.6 58.0 %shard_map.77 = (f32[2,8,16,16,128]{4,3,2,1,0:T(8,128)}, f32[16,256]{1,0:T(8,128)}) custom-call(bf16[2,8,16,16,128]{4,3,2,1,0:T(8,128)(2,1)} %refs_0_.1, bf16[8,16,16,512]{3,2,1,0:T(8,128)(2,1)} %refs_1_.1, f32[8,16,16]{2,1,0:T(8,128)} %refs_2_.1, f32[8,16,16]{2,1,0:T(8,128)} %refs_3_.1, bf16[729,729]{1,0:T(8,128)(2,1)} %refs_4_.1, s32[1,1,4,729]{3,2,1,0:T(4,128)} %refs_5_.1), custom_call_target="tpu_custom_call" | custom-call | tf_op jit(solution)/shard_map/pallas_call | solution.py:425
  58.6 2.4 %shard_map.78 = (f32[2,8,16,16,128]{4,3,2,1,0:T(8,128)}, f32[16,256]{1,0:T(8,128)}) custom-call(f32[2,8,16,16,128]{4,3,2,1,0:T(8,128)} %get-tuple-element.4.values, f32[16,256]{1,0:T(8,128)} %get-tuple-element.5.rows), custom_call_target="tpu_custom_call" | custom-call | tf_op jit(solution)/shard_map/pallas_call | solution.py:484

commit v7 on v5

--- a/solution.py
+++ b/solution.py
@@ -26,7 +26,7 @@
     vec, mass, pot, amat, conn,
     ap, ac, acc, uf, y, im, bt, ub, wp, mloc, rs, rt, vb, posr, ct,
     xh, yh, dh, cx, cy_, cd, sx, sy, rx, ry, rd,
-    m1s, m1r, m2s, m2r, m3f, m3s, m3r, m4s, m4r,
+    m1s, m1r, m2s, m2r, m3s, m3r, m4s, m4r,
     hs_sem, hr_sem, es_sem, er_sem, s1, r1, s2, r2, s3, r3, s4, r4, osem, lsem,
 ):
     p = lax.axis_index("dx")
@@ -191,48 +191,64 @@
             if n in wanted
         ]
 
-    def cells(d, b):
+    def gather(b, c):
+        cy, cz = c // 2, c % 2
         flat = uf.at[b].reshape(EX * EY * EZ, W)
+        kp = (8 * cz + 8) % 16
+        main = uf[b, :, 8 * cy : 8 * cy + 9, 8 * cz : 8 * cz + 8, :].reshape(648, W)
+        planes = [flat[pl.ds((i * EY + 8 * cy) * EZ + kp, 8, EZ), :] for i in range(EX)]
+        start = (8 * cy + 8) * EZ + kp
+        line = flat[pl.ds(start, 8, EY * EZ), :]
+        last = flat[pl.ds(start + 8 * EY * EZ, 1), :]
+        first = lax.broadcasted_iota(jnp.int32, (8, W), 0) == 0
+        last = jnp.where(first, jnp.broadcast_to(last, (8, W)), 0.0)
+        whole = jnp.concatenate([main] + planes + [line, last, jnp.zeros((32, W), F32)], axis=0)
+        ub[c, :, b * W : (b + 1) * W] = whole.astype(BF16)
+
+    def place(b, c, w):
+        cy, cz = c // 2, c % 2
+        ks = slice(8 * cz, 8 * cz + 8)
+        wp[b, c] = w[648:]
+        block = w[:648].reshape(EX, 9, 8, W)
+        if cy == 0:
+            acc[b, :, 0:9, ks, :] = block
+        else:
+            acc[b, :, 8, ks, :] += block[:, 0]
+            acc[b, :, 9:17, ks, :] = block[:, 1:]
+
+    def planes_of(b, c):
+        cy, cz = c // 2, c % 2
         total = acc.at[b].reshape(EX * EY * EZ, W)
+        kp = (8 * cz + 8) % 16
+        for i in range(EX):
+            where = pl.ds((i * EY + 8 * cy) * EZ + kp, 8, EZ)
+            total[where, :] = total[where, :] + wp[b, c, 8 * i : 8 * i + 8]
+        start = (8 * cy + 8) * EZ + kp
+        where = pl.ds(start, 8, EY * EZ)
+        total[where, :] = total[where, :] + wp[b, c, 72:80]
+        where = pl.ds(start + 8 * EY * EZ, 1)
+        total[where, :] = total[where, :] + wp[b, c, 80:81]
+
+    def cells(d, blocks):
+        cols = slice(blocks[0] * W, (blocks[-1] + 1) * W)
         for cy in range(2):
             for cz in range(2):
                 c = cy * 2 + cz
-                kp = (8 * cz + 8) % 16
-                ks = slice(8 * cz, 8 * cz + 8)
-                main = uf[b, :, 8 * cy : 8 * cy + 9, ks, :].reshape(648, W)
-                planes = [flat[pl.ds((i * EY + 8 * cy) * EZ + kp, 8, EZ), :] for i in range(EX)]
-                start = (8 * cy + 8) * EZ + kp
-                line = flat[pl.ds(start, 8, EY * EZ), :]
-                last = flat[pl.ds(start + 8 * EY * EZ, 1), :]
-                first = lax.broadcasted_iota(jnp.int32, (8, W), 0) == 0
-                last = jnp.where(first, jnp.broadcast_to(last, (8, W)), 0.0)
-                whole = jnp.concatenate([main] + planes + [line, last, jnp.zeros((32, W), F32)], axis=0)
-                ub[b, c] = whole.astype(BF16)
-                w = jnp.dot(ac[c], ub[b, c], preferred_element_type=F32)
-                wp[b, c] = w[648:]
-                block = w[:648].reshape(EX, 9, 8, W)
-                if cy == 0:
-                    acc[b, :, 0:9, ks, :] = block
-                else:
-                    acc[b, :, 8, ks, :] += block[:, 0]
-                    acc[b, :, 9:17, ks, :] = block[:, 1:]
+                for b in blocks:
+                    gather(b, c)
+                w = jnp.dot(ac[c], ub[c, :, cols], preferred_element_type=F32)
+                for n, b in enumerate(blocks):
+                    place(b, c, w[:, n * W : (n + 1) * W])
             for cz in range(2):
-                c = cy * 2 + cz
-                kp = (8 * cz + 8) % 16
-                for i in range(EX):
-                    where = pl.ds((i * EY + 8 * cy) * EZ + kp, 8, EZ)
-                    total[where, :] = total[where, :] + wp[b, c, 8 * i : 8 * i + 8]
-                start = (8 * cy + 8) * EZ + kp
-                where = pl.ds(start, 8, EY * EZ)
-                total[where, :] = total[where, :] + wp[b, c, 72:80]
-                where = pl.ds(start + 8 * EY * EZ, 1)
-                total[where, :] = total[where, :] + wp[b, c, 80:81]
-        sx[d, 0, b] = acc[b, 0].astype(BF16)
-        sx[d, 1, b] = acc[b, LO].astype(BF16)
-        sy[d, 0, b] = acc[b, :, 0].astype(BF16)
-        sy[d, 1, b] = acc[b, :, 16].astype(BF16)
-        for copy in exchange(d, b):
-            copy.start()
+                for b in blocks:
+                    planes_of(b, cy * 2 + cz)
+        for b in blocks:
+            sx[d, 0, b] = acc[b, 0].astype(BF16)
+            sx[d, 1, b] = acc[b, LO].astype(BF16)
+            sy[d, 0, b] = acc[b, :, 0].astype(BF16)
+            sy[d, 1, b] = acc[b, :, 16].astype(BF16)
+            for copy in exchange(d, b):
+                copy.start()
 
     def update(d, b):
         now, later = d % 2, (d + 1) % 2
@@ -329,7 +345,10 @@
                 for side in range(2):
                     y[side, b, LO] = jnp.zeros((EY, EZ, W), F32)
                     y[side, b, 0:LO, 16] = jnp.zeros((LO, EZ, W), F32)
-            cells(d, b)
+            if d > 0:
+                cells(d, (b,))
+            elif b == 0:
+                cells(d, tuple(range(BLOCKS)))
             if d == 0 and b == BLOCKS - 1:
                 for copy in rhalo[2:]:
                     copy.start()
@@ -360,8 +379,7 @@
             for k in range(NXC - 1):
                 total = total + m2r[b, k, zv].astype(F32)
             for half in range(ZL):
-                m3f[zv * ZL + half, :, b * W : (b + 1) * W] = total[half * 8 : half * 8 + 8]
-                m3s[zv * ZL + half, :, b * W : (b + 1) * W] = total[half * 8 : half * 8 + 8].astype(BF16)
+                m3s[zv * ZL + half, :, b * W : (b + 1) * W] = total[half * 8 : half * 8 + 8]
     copies = [
         remote(m3s.at[(zi + k + 1) % nz], m3r.at[k], s3.at[k], r3.at[k], column[k]) for k in range(nz - 1)
     ]
@@ -369,9 +387,9 @@
         copy.start()
     for copy in copies:
         copy.wait()
-    total = m3f[zi]
+    total = m3s[zi]
     for k in range(nz - 1):
-        total = total + m3r[k].astype(F32)
+        total = total + m3r[k]
     m4s[...] = total
     m4r[p] = total
     copies = [remote(m4s, m4r.at[p], s4.at[k], r4.at[k], group[k]) for k in range(ndx - 1)]
@@ -423,7 +441,7 @@
             pltpu.VMEM((2, *state), F32),
             pltpu.VMEM((EX, EY, EZ, W), F32),
             pltpu.VMEM((EX, EY, EZ, W), F32),
-            pltpu.VMEM((BLOCKS, NCELL, KP, W), BF16),
+            pltpu.VMEM((NCELL, KP, BLOCKS * W), BF16),
             pltpu.VMEM((BLOCKS, NCELL, KP - 648, W), F32),
             pltpu.VMEM((BLOCKS, rows, W), F32),
             pltpu.VMEM((EX, EY, EZ, nres), BF16),
@@ -447,8 +465,7 @@
             pltpu.VMEM((BLOCKS, NXC - 1, ZH, 16, W), BF16),
             pltpu.VMEM((BLOCKS, NXC - 1, ZH, 16, W), BF16),
             pltpu.VMEM((nz, 8, BLOCKS * W), F32),
-            pltpu.VMEM((nz, 8, BLOCKS * W), BF16),
-            pltpu.VMEM((nz - 1, 8, BLOCKS * W), BF16),
+            pltpu.VMEM((nz - 1, 8, BLOCKS * W), F32),
             pltpu.VMEM((8, BLOCKS * W), F32),
             pltpu.VMEM((ndx, 8, BLOCKS * W), F32),
             dma((10,)), dma((10,)), dma((DEGREE, BLOCKS, 8)), dma((DEGREE, BLOCKS, 8)),

time: 61.3 us -> 61.6 us (level)
  no operation moved by 1% of the time
where the time goes in v7:
time: 61.6 us; the launch traced here: 61 us
  Pallas kernels  60.2 us (98%)
  between operations  0.8 us (1%)
    pallas_call x1, Pallas kernels, body(): pl.pallas_call(k, out_shape=(jax.ShapeDtypeStruct((BLOCKS, LO, 16, EZ, W)...  57.7 us
    pallas_call x1, Pallas kernels, body(): pl.pallas_call(hand_on, out_shape=tuple((jax.ShapeDtypeStruct(r.shape, F3...  2.43 us

profile of v7, /device:TPU:4, one launch (start us, length us, event | category | flops | bytes accessed | tf_op | source)
XLA Modules:
  0.0 61.0 jit_solution(5315796889867220280)
XLA Ops:
  0.6 57.7 %shard_map.77 = (f32[2,8,16,16,128]{4,3,2,1,0:T(8,128)}, f32[16,256]{1,0:T(8,128)}) custom-call(bf16[2,8,16,16,128]{4,3,2,1,0:T(8,128)(2,1)} %refs_0_.1, bf16[8,16,16,512]{3,2,1,0:T(8,128)(2,1)} %refs_1_.1, f32[8,16,16]{2,1,0:T(8,128)} %refs_2_.1, f32[8,16,16]{2,1,0:T(8,128)} %refs_3_.1, bf16[729,729]{1,0:T(8,128)(2,1)} %refs_4_.1, s32[1,1,4,729]{3,2,1,0:T(4,128)} %refs_5_.1), custom_call_target="tpu_custom_call" | custom-call | tf_op jit(solution)/shard_map/pallas_call | solution.py:423
  58.4 2.4 %shard_map.78 = (f32[2,8,16,16,128]{4,3,2,1,0:T(8,128)}, f32[16,256]{1,0:T(8,128)}) custom-call(f32[2,8,16,16,128]{4,3,2,1,0:T(8,128)} %get-tuple-element.4.values, f32[16,256]{1,0:T(8,128)} %get-tuple-element.5.rows), custom_call_target="tpu_custom_call" | custom-call | tf_op jit(solution)/shard_map/pallas_call | solution.py:480
